TPU v7x, 32 devices: a whole 2x2x4 slice. The times are simulated.
32 devices in a mesh: gx: 2 (over x), gy: 4 (over z), gz: 4 (over y, core).
Axes of the slice: x: 2, y: 2, z: 4, core: 2. Of those that a mesh axis runs over, the one named last changes fastest.
Arguments:
- particle_mass: float32 [1048576], P(('gx', 'gy', 'gz')), may hold values from 0.5 to 2
- particle_velocity: float32 [3, 1048576], P(None, ('gx', 'gy', 'gz')), may hold values from -6 to 6
- particle_affine: float32 [9, 1048576], P(None, ('gx', 'gy', 'gz')), may hold values from -6 to 6
- particle_cell: int32 [3, 1048576], P(None, ('gx', 'gy', 'gz')), may hold values from 0 to 13
- particle_fraction: int32 [3, 1048576], P(None, ('gx', 'gy', 'gz')), may hold values from 0 to 1023
- block_owner: int32 [2048, 1], P(('gx', 'gy', 'gz')), may hold values from 0 to 15; in each aligned block of 64 rows (0 to 63, 64 to 127, ...) at most 8 rows name the same one
- block_slot: int32 [2048], P(('gx', 'gy', 'gz')), may hold values from 0 to 31
- block_count: int32 [2048], P(('gx', 'gy', 'gz')), may hold values from 128 to 512
- cell_drag: float32 [1024, 4096], P(('gx', 'gy', 'gz')), may hold values from 0.5 to 2
Outputs:
- grid_velocity: float32 [1024, 3, 4096], P(('gx', 'gy', 'gz'))
- new_velocity: float32 [3, 1048576], P(None, ('gx', 'gy', 'gz'))
- new_affine: float32 [9, 1048576], P(None, ('gx', 'gy', 'gz'))
Inputs may be any that keep to these rules, and one draw needn't show every extreme that they name: `block_owner`: owner index counted over the devices with the particle device's own gx index, in gy+gz order; among the rows of one device, no owner is named more than 8 times. `block_count`: slots at or beyond the count are absent. `particle_cell`: A particle's three stencil nodes lie inside its grid block.
All inputs are finite; a program needn't handle non-finite values.
Results may differ from a plain program's by a relative error of at most 0.0085.
Values may be sent and summed in bfloat16 or wider, within the bound.
A program may use at most 128 MiB of HBM per device.

v0:
```python
import functools

import jax
import jax.numpy as jnp
from jax import lax
from jax.experimental import pallas as pl
from jax.experimental.pallas import tpu as pltpu
from jax.sharding import PartitionSpec as P

EDGE = 16
QUANT = 1024
LANES = 128
FIELDS = 20
RESULTS = 12
UNROLL = 4
HALVES = 2
GROUP_AXES = ("gy", "gz")
F32 = jnp.float32
BF16 = jnp.bfloat16


SMEM = pl.BlockSpec(memory_space=pltpu.SMEM)
VMEM = pl.BlockSpec(memory_space=pltpu.VMEM)
PARAMS = pltpu.CompilerParams(vmem_limit_bytes=20 << 20)


def cost(flops):
    return pl.CostEstimate(flops=flops, bytes_accessed=1 << 22, transcendentals=0)


def pack_kernel(
    portion,
    owner_ref,
    slot_ref,
    count_ref,
    mass_ref,
    velocity_ref,
    affine_ref,
    cell_ref,
    fraction_ref,
    *rest,
):
    payload_refs, (dest_ref, used_ref, stage_ref), staged, sems = (
        rest[:-9],
        rest[-9:-6],
        rest[-6:-1],
        rest[-1],
    )
    sources = (mass_ref, velocity_ref, affine_ref, cell_ref, fraction_ref)
    copies = [
        pltpu.make_async_copy(source, target, sems.at[i])
        for i, (source, target) in enumerate(zip(sources, staged))
    ]
    for copy in copies:
        copy.start()
    mass_ref, velocity_ref, affine_ref, cell_ref, fraction_ref = staged
    blocks = owner_ref.shape[0]
    group_size = used_ref.shape[0]
    width = mass_ref.shape[1]
    half_rows = payload_refs[0].shape[1]
    half_width = width // HALVES

    def clear_used(i, carry):
        used_ref[i] = 0
        return carry

    lax.fori_loop(0, group_size, clear_used, 0)
    lane = lax.broadcasted_iota(jnp.int32, (1, width), 1)

    def clear_marks(i, carry):
        for payload_ref in payload_refs:
            payload_ref[i, 16:32, :] = jnp.full((16, LANES), -1.0, BF16)
        return carry

    lax.fori_loop(0, payload_refs[0].shape[0], clear_marks, 0)
    for copy in copies:
        copy.wait()

    def pack(block, carry):
        owner = owner_ref[block]
        rank = used_ref[owner]
        used_ref[owner] = rank + 1
        chunk = rank // portion
        where = owner * portion + rank % portion
        dest_ref[block] = chunk * (group_size * portion) + where
        count = count_ref[block]
        mark = slot_ref[block].astype(F32)
        cols = pl.ds(pl.multiple_of(block * width, LANES), width)
        live = jnp.where(lane < count, mass_ref[pl.ds(block, 1), :], 0.0)
        velocity = velocity_ref[:, cols]
        affine = affine_ref[:, cols]
        code = cell_ref[:, cols] * QUANT + fraction_ref[:, cols]
        high = (code >> 7).astype(F32)
        low = (code & 127).astype(F32)
        for q in range(width // LANES):
            part = slice(q * LANES, (q + 1) * LANES)
            first_lane = q * LANES // half_width * half_width
            base = q * FIELDS
            stage_ref[base : base + 1] = live[:, part]
            stage_ref[base + 1 : base + 4] = velocity[:, part]
            stage_ref[base + 4 : base + 13] = affine[:, part]
            stage_ref[base + 13 : base + 16] = high[:, part]
            stage_ref[base + 16 : base + 19] = low[:, part]
            stage_ref[base + 19 : base + 20] = jnp.full(
                (1, LANES), jnp.where(count > first_lane, mark, -1.0), F32
            )
        for c, payload_ref in enumerate(payload_refs):

            @pl.when(chunk == c)
            def _():
                for h in range(HALVES):
                    payload_ref[where * HALVES + h] = stage_ref[
                        h * half_rows : (h + 1) * half_rows
                    ].astype(BF16)

        return carry

    lax.fori_loop(0, blocks, pack, 0)


def pack(chunks, portion, group_size, owner, slot, count, mass, velocity, affine, cell, fraction):
    blocks = owner.shape[0]
    width = mass.shape[0] // blocks
    rows = width // LANES * FIELDS
    payload = jax.ShapeDtypeStruct(
        (group_size * portion * HALVES, rows // HALVES, LANES), BF16
    )
    arrays = (mass.reshape(blocks, width), velocity, affine, cell, fraction)
    outs = pl.pallas_call(
        functools.partial(pack_kernel, portion),
        name="pack",
        out_shape=(payload,) * chunks + (jax.ShapeDtypeStruct((blocks,), jnp.int32),),
        in_specs=[SMEM] * 3 + [pl.BlockSpec(memory_space=pltpu.HBM)] * 5,
        out_specs=(VMEM,) * chunks + (SMEM,),
        scratch_shapes=[pltpu.SMEM((group_size,), jnp.int32), pltpu.VMEM((rows, LANES), F32)]
        + [pltpu.VMEM(array.shape, array.dtype) for array in arrays]
        + [pltpu.SemaphoreType.DMA((len(arrays),))],
        compiler_params=pltpu.CompilerParams(vmem_limit_bytes=60 << 20),
    )(owner, slot, count, *arrays)
    return outs[:-1], outs[-1]


def twice(rows):
    return jnp.concatenate([rows, rows], axis=0)


def load_item(u, item_ref, fields_ref):
    rows = item_ref.shape[0]
    quarters = rows // FIELDS
    first = u * rows
    fields_ref[first : first + rows] = item_ref[...].astype(F32)
    for q in range(quarters):
        base = first + q * FIELDS
        fields_ref[base + 13 : base + 16] = (
            fields_ref[base + 13 : base + 16] * (128.0 / QUANT)
            + fields_ref[base + 16 : base + 19] * (1.0 / QUANT)
            + (0.5 + 0.5 / QUANT)
        )

    def spread(field):
        return twice(
            jnp.concatenate(
                [
                    fields_ref[pl.ds(first + q * FIELDS + field, 8, stride=0), :]
                    for q in range(quarters)
                ],
                axis=1,
            )
        )

    return spread, quarters


def stencil(spread, node, dim):
    offset = node - spread(13 + dim)
    magnitude = jnp.abs(offset)
    outer_part = jnp.maximum(1.5 - magnitude, 0.0)
    weight = jnp.where(
        magnitude < 0.5, 0.75 - magnitude * magnitude, 0.5 * outer_part * outer_part
    )
    return weight, weight * offset


def planes(u, spread, quarters, node, rows_ref):
    factors_y = stencil(spread, node, 1)
    factors_z = [factor.astype(BF16) for factor in stencil(spread, node, 2)]
    firsts = [(u * 2 + k) * quarters * EDGE for k in range(2)]
    for first, factor in zip(firsts, factors_y):
        for q in range(quarters):
            rows_ref[first + q * EDGE : first + (q + 1) * EDGE] = factor[
                :, q * LANES : (q + 1) * LANES
            ]

    def row(first, y):
        return jnp.concatenate(
            [
                twice(rows_ref[pl.ds(first + q * EDGE + y, 8, stride=0), :]).astype(BF16)
                for q in range(quarters)
            ],
            axis=1,
        )

    zero, one, two = [], [], []
    for y in range(EDGE):
        weight_row, slope_row = row(firsts[0], y), row(firsts[1], y)
        zero.append(weight_row * factors_z[0])
        one.append(slope_row * factors_z[0])
        two.append(weight_row * factors_z[1])
    return [jnp.concatenate(parts, axis=0) for parts in (zero, one, two)]


def nodes(quarters):
    return lax.broadcasted_iota(jnp.int32, (EDGE, quarters * LANES), 0).astype(F32)


def deposit(u, item_ref, fields_ref, rows_ref):
    spread, quarters = load_item(u, item_ref, fields_ref)
    node = nodes(quarters)
    weight_x, slope_x = stencil(spread, node, 0)
    mass = spread(0)
    mass_x = mass * weight_x
    mass_slope = mass * slope_x
    nothing = jnp.zeros(mass_x.shape, BF16)
    lead_zero, lead_one, lead_two = [mass_x.astype(BF16)], [nothing], [nothing]
    for d in range(3):
        lead_zero.append(
            (spread(1 + d) * mass_x + spread(4 + 3 * d) * mass_slope).astype(BF16)
        )
        lead_one.append((spread(5 + 3 * d) * mass_x).astype(BF16))
        lead_two.append((spread(6 + 3 * d) * mass_x).astype(BF16))
    lead = jnp.concatenate(
        [jnp.concatenate(part, axis=0) for part in (lead_zero, lead_one, lead_two)], axis=1
    )
    plane = jnp.concatenate(planes(u, spread, quarters, node, rows_ref), axis=1)
    return lax.dot_general(lead, plane, (((1,), (1,)), ((), ())), preferred_element_type=F32)


def interpolate(u, item_ref, grid_rows, fields_ref, rows_ref, parts_ref):
    spread, quarters = load_item(u, item_ref, fields_ref)
    node = nodes(quarters)
    weight_x, slope_x = stencil(spread, node, 0)
    moments = [
        jnp.dot(grid_rows, plane, preferred_element_type=F32)
        for plane in planes(u, spread, quarters, node, rows_ref)
    ]
    slope_four = 4.0 * slope_x
    weight_four = 4.0 * weight_x
    first = u * quarters * RESULTS * 8
    for d in range(3):
        span = slice(d * EDGE, (d + 1) * EDGE)
        entries = (
            (d, weight_x, moments[0]),
            (3 + 3 * d, slope_four, moments[0]),
            (4 + 3 * d, weight_four, moments[1]),
            (5 + 3 * d, weight_four, moments[2]),
        )
        for entry, factor, moment in entries:
            product = factor * moment[span]
            partial = product[:8] + product[8:]
            for q in range(quarters):
                at = first + (q * RESULTS + entry) * 8
                parts_ref[at : at + 8] = partial[:, q * LANES : (q + 1) * LANES]
    groups = []
    for g in range(quarters * RESULTS // 8):
        total = parts_ref[pl.ds(first + g * 64, 8, stride=8), :]
        for j in range(1, 8):
            total = total + parts_ref[pl.ds(first + g * 64 + j, 8, stride=8), :]
        groups.append(total)
    return jnp.concatenate(groups, axis=0).astype(BF16)


def collect_filled(tiles_ref, order_ref):
    def collect(s, filled):
        order_ref[filled] = s
        return filled + (tiles_ref[s] >= 0).astype(jnp.int32)

    order_ref[0] = 0
    filled = lax.fori_loop(0, tiles_ref.shape[0], collect, 0)
    last = order_ref[jnp.maximum(filled - 1, 0)]
    for u in range(UNROLL):
        order_ref[filled + u] = last
    return filled


def scatter_items(tiles_ref, arrived_ref, sums_ref, order_ref, fields_ref, rows_ref):
    filled = collect_filled(tiles_ref, order_ref)
    spare = sums_ref.shape[0] - 1

    def scatter(step, carry):
        results = []
        for u in range(UNROLL):
            at = step * UNROLL + u
            s = order_ref[at]
            tile = jnp.where(at < filled, tiles_ref[s], spare)
            results.append((tile, deposit(u, arrived_ref.at[s], fields_ref, rows_ref)))
        for tile, sums in results:
            sums_ref[tile] += sums
        return carry

    lax.fori_loop(0, (filled + UNROLL - 1) // UNROLL, scatter, 0)


def gather_items(
    tiles_ref, arrived_ref, round_ref, out_ref, order_ref, fields_ref, rows_ref, parts_ref
):
    filled = collect_filled(tiles_ref, order_ref)

    def gather(step, carry):
        for u in range(UNROLL):
            s = order_ref[step * UNROLL + u]
            out_ref[s] = interpolate(
                u,
                arrived_ref.at[s],
                round_ref[jnp.maximum(tiles_ref[s], 0)],
                fields_ref,
                rows_ref,
                parts_ref,
            )
        return carry

    lax.fori_loop(0, (filled + UNROLL - 1) // UNROLL, gather, 0)


def work_shapes(slots, item_rows):
    quarters = item_rows // FIELDS
    return [
        pltpu.SMEM((slots + UNROLL,), jnp.int32),
        pltpu.VMEM((UNROLL * item_rows, LANES), F32),
        pltpu.VMEM((UNROLL * 2 * quarters * EDGE, LANES), F32),
        pltpu.VMEM((UNROLL * quarters * RESULTS * 8, LANES), F32),
    ]


def start_kernel(drag_ref, sums_ref):
    plane_size = EDGE * EDGE

    def start(t, carry):
        for x in range(EDGE):
            sums_ref[t, x : x + 1, :] = drag_ref[
                pl.ds(t, 1), x * plane_size : (x + 1) * plane_size
            ]
        sums_ref[t, EDGE:, :] = jnp.zeros((3 * EDGE, plane_size), F32)
        return carry

    lax.fori_loop(0, drag_ref.shape[0], start, 0)
    sums_ref[drag_ref.shape[0]] = jnp.zeros((4 * EDGE, plane_size), F32)


def start_sums(drag):
    return pl.pallas_call(
        start_kernel,
        name="start_sums",
        out_shape=jax.ShapeDtypeStruct((drag.shape[0] + 1, 4 * EDGE, EDGE * EDGE), F32),
        in_specs=[VMEM],
        out_specs=VMEM,
        compiler_params=PARAMS,
        cost_estimate=cost(1 << 20),
    )(drag)


def copy_sums(before_ref, sums_ref):
    def copy(t, carry):
        sums_ref[t] = before_ref[t]
        return carry

    lax.fori_loop(0, sums_ref.shape[0], copy, 0)


def scatter_kernel(
    tiles_ref, arrived_ref, before_ref, sums_ref, order_ref, fields_ref, rows_ref, parts_ref
):
    copy_sums(before_ref, sums_ref)
    scatter_items(tiles_ref, arrived_ref, sums_ref, order_ref, fields_ref, rows_ref)


def scatter_step(tiles, arrived, sums):
    return pl.pallas_call(
        scatter_kernel,
        name="scatter_step",
        out_shape=jax.ShapeDtypeStruct(sums.shape, F32),
        in_specs=[SMEM, VMEM, VMEM],
        out_specs=VMEM,
        scratch_shapes=work_shapes(arrived.shape[0], arrived.shape[1]),
        compiler_params=PARAMS,
        cost_estimate=cost(10**10),
    )(tiles, arrived, sums)


def grid_kernel(
    last_tiles_ref,
    last_ref,
    tiles_ref,
    arrived_ref,
    before_ref,
    grid_ref,
    round_ref,
    out_ref,
    order_ref,
    fields_ref,
    rows_ref,
    parts_ref,
    sums_ref,
):
    plane_size = EDGE * EDGE
    copy_sums(before_ref, sums_ref)
    scatter_items(last_tiles_ref, last_ref, sums_ref, order_ref, fields_ref, rows_ref)

    def divide(t, carry):
        mass = sums_ref[t, :EDGE, :]
        parts = [sums_ref[t, (d + 1) * EDGE : (d + 2) * EDGE, :] / mass for d in range(3)]
        round_ref[t] = jnp.concatenate(parts, axis=0).astype(BF16)
        for d in range(3):
            for x in range(EDGE):
                grid_ref[d, pl.ds(t, 1), x * plane_size : (x + 1) * plane_size] = parts[d][
                    x : x + 1
                ]
        return carry

    lax.fori_loop(0, round_ref.shape[0], divide, 0)
    gather_items(
        tiles_ref, arrived_ref, round_ref, out_ref, order_ref, fields_ref, rows_ref, parts_ref
    )


def result_shape(arrived):
    slots, rows, _ = arrived.shape
    return jax.ShapeDtypeStruct((slots, rows // FIELDS * RESULTS, LANES), BF16)


def grid_step(last_tiles, last, tiles, arrived, sums):
    tile_count = sums.shape[0] - 1
    plane_size = EDGE * EDGE
    return pl.pallas_call(
        grid_kernel,
        name="grid_step",
        out_shape=(
            jax.ShapeDtypeStruct((3, tile_count, EDGE * plane_size), F32),
            jax.ShapeDtypeStruct((tile_count, 3 * EDGE, plane_size), BF16),
            result_shape(arrived),
        ),
        in_specs=[SMEM, VMEM, SMEM, VMEM, VMEM],
        out_specs=(VMEM,) * 3,
        scratch_shapes=work_shapes(arrived.shape[0], arrived.shape[1])
        + [pltpu.VMEM(sums.shape, F32)],
        compiler_params=PARAMS,
        cost_estimate=cost(10**10),
    )(last_tiles, last, tiles, arrived, sums)


def gather_step(tiles, arrived, rounded):
    return pl.pallas_call(
        gather_items,
        name="gather_step",
        out_shape=result_shape(arrived),
        in_specs=[SMEM, VMEM, VMEM],
        out_specs=VMEM,
        scratch_shapes=work_shapes(arrived.shape[0], arrived.shape[1]),
        compiler_params=PARAMS,
        cost_estimate=cost(10**10),
    )(tiles, arrived, rounded)


def unpack_kernel(dest_ref, count_ref, *refs):
    returned_refs, (velocity_ref, affine_ref) = refs[:-2], refs[-2:]
    blocks = dest_ref.shape[0]
    width = velocity_ref.shape[1] // blocks
    slots = returned_refs[0].shape[0] // HALVES
    half_width = width // HALVES
    lane = lax.broadcasted_iota(jnp.int32, (1, LANES), 1)

    def unpack(block, carry):
        dest = dest_ref[block]
        count = count_ref[block]
        for c, returned_ref in enumerate(returned_refs):

            @pl.when(dest // slots == c)
            def _():
                for h in range(HALVES):
                    rows = returned_ref[(dest - c * slots) * HALVES + h].astype(F32)
                    for q in range(half_width // LANES):
                        first = h * half_width + q * LANES
                        cols = pl.ds(pl.multiple_of(block * width + first, LANES), LANES)
                        part = jnp.where(
                            lane + first < count, rows[q * RESULTS : (q + 1) * RESULTS], 0.0
                        )
                        velocity_ref[:, cols] = part[:3]
                        affine_ref[:, cols] = part[3:]

        return carry

    lax.fori_loop(0, blocks, unpack, 0)


def unpack(dest, count, returned, width):
    particles = dest.shape[0] * width
    return pl.pallas_call(
        unpack_kernel,
        name="unpack",
        out_shape=(
            jax.ShapeDtypeStruct((3, particles), F32),
            jax.ShapeDtypeStruct((9, particles), F32),
        ),
        in_specs=[SMEM, SMEM] + [VMEM] * len(returned),
        out_specs=(VMEM, VMEM),
        compiler_params=PARAMS,
    )(dest, count, *returned)


def tile_marks(arrived):
    return arrived[:, FIELDS - 1, 0].astype(jnp.int32)


def exchange(value):
    return lax.all_to_all(value, GROUP_AXES, split_axis=0, concat_axis=0, tiled=True)


def per_device(
    particle_mass,
    particle_velocity,
    particle_affine,
    particle_cell,
    particle_fraction,
    block_owner,
    block_slot,
    block_count,
    cell_drag,
):
    group_size = lax.axis_size(GROUP_AXES)
    blocks = block_count.shape[0]
    capacity = max(1, 2 * blocks // group_size)
    chunks = 2 if capacity % 2 == 0 else 1
    portion = capacity // chunks
    payloads, dest = pack(
        chunks,
        portion,
        group_size,
        block_owner[:, 0],
        block_slot,
        block_count,
        particle_mass,
        particle_velocity,
        particle_affine,
        particle_cell,
        particle_fraction,
    )
    arrived = [exchange(payloads[0])]
    for payload in payloads[1:]:
        arrived[-1], payload = lax.optimization_barrier((arrived[-1], payload))
        arrived.append(exchange(payload))
    tiles = [tile_marks(part) for part in arrived]
    sums = start_sums(cell_drag)
    for c in range(chunks - 1):
        sums = scatter_step(tiles[c], arrived[c], sums)
    grid_velocity, rounded, results = grid_step(
        tiles[-1], arrived[-1], tiles[0], arrived[0], sums
    )
    returned = [exchange(results)]
    for c in range(1, chunks):
        returned.append(exchange(gather_step(tiles[c], arrived[c], rounded)))
    new_velocity, new_affine = unpack(
        dest, block_count, returned, particle_mass.shape[0] // blocks
    )
    return jnp.transpose(grid_velocity, (1, 0, 2)), new_velocity, new_affine


def solution(mesh):
    everywhere = ("gx", "gy", "gz")
    return jax.shard_map(
        per_device,
        mesh=mesh,
        in_specs=(
            P(everywhere),
            P(None, everywhere),
            P(None, everywhere),
            P(None, everywhere),
            P(None, everywhere),
            P(everywhere, None),
            P(everywhere),
            P(everywhere),
            P(everywhere, None),
        ),
        out_specs=(P(everywhere, None, None), P(None, everywhere), P(None, everywhere)),
        check_vma=False,
    )
```

profile of v0, /device:TPU:0, one launch (start us, length us, event | category | flops | bytes accessed | tf_op | source)
XLA Modules:
  0.0 173.4 jit_solution(10313813598193862064)
XLA Ops:
  0.6 1.6 reshape.13.mass_ref
  2.2 6.4 %pack.1 = (bf16[128,40,128]{2,1,0:T(8,128)(2,1)}, bf16[128,40,128]{2,1,0:T(8,128)(2,1)}, s32[64]{0:T(128)}) custom-call(s32[64]{0:T(128)} %bitcast.2, s32[64]{0:T(128)} %slot_ref.1, s32[64]{0:T(128)} %count_ref.3, f32[64,512]{1,0:T(8,128)} %reshape.13.mass_ref, f32[3,32768]{1,0:T(4,128)} %velocity_ref.1, f32[9,32768]{1,0:T(8,128)} %affine_ref.1, ...), custom_call_target="tpu_custom_call" | custom-call | tf_op jit(solution)/shard_map/pack/pallas_call | solution.py:129
  8.6 38.8 %all_to_all.20.arrived_ref = bf16[128,40,128]{2,1,0:T(8,128)(2,1)S(1)} all-to-all(bf16[128,40,128]{2,1,0:T(8,128)(2,1)} %get-tuple-element.13), channel_id=1, replica_groups=mesh['gx'=2,'gy'=4,'gz'=4] {'gy','gz'}, dimensions={0} | all-to-all | bytes 2621440 | tf_op jit(solution)/shard_map/all_to_all | solution.py:514
  47.4 0.0 copy-start
  47.4 4.1 %all-to-all-start.1 = ((bf16[128,40,128]{2,1,0:T(8,128)(2,1)}), bf16[128,40,128]{2,1,0:T(8,128)(2,1)S(1)}, u32[]{:S(2)}, u32[]{:S(2)}) async-start(bf16[128,40,128]{2,1,0:T(8,128)(2,1)} %get-tuple-element.15), calls=%async_computation.1 | async-start | bytes 2621440 | tf_op jit(solution)/shard_map/all_to_all | solution.py:514
  51.6 0.0 copy-done
  51.6 0.5 start_sums.1.before_ref
  52.1 2.4 %convert_reduce_fusion.tiles_ref = s32[128]{0:T(128)S(1)} fusion(bf16[128,40,128]{2,1,0:T(8,128)(2,1)S(1)} %all_to_all.20.arrived_ref), kind=kLoop, calls=%fused_computation.2 | loop fusion | flops 128 | bytes 768 | tf_op jit(solution)/shard_map/convert_element_type | solution.py:510
  54.4 18.6 %scatter_step.1.before_ref = f32[33,64,256]{2,1,0:T(8,128)S(1)} custom-call(s32[128]{0:T(128)S(1)} %convert_reduce_fusion.tiles_ref, bf16[128,40,128]{2,1,0:T(8,128)(2,1)S(1)} %all_to_all.20.arrived_ref, f32[33,64,256]{2,1,0:T(8,128)S(1)} %start_sums.1.before_ref), custom_call_target="tpu_custom_call" | custom-call | flops 10000000000 | bytes 4194304 | tf_op jit(solution)/shard_map/scatter_step/pallas_call | solution.py:377
  73.0 0.0 copy-start.3
  73.1 1.3 copy-done.3
  74.4 4.5 %all-to-all-done.1.last_ref.arrived_ref = bf16[128,40,128]{2,1,0:T(8,128)(2,1)S(1)} async-done(((bf16[128,40,128]{2,1,0:T(8,128)(2,1)}), bf16[128,40,128]{2,1,0:T(8,128)(2,1)S(1)}, u32[]{:S(2)}, u32[]{:S(2)}) %all-to-all-start.1) | async-done | bytes 1310752 | tf_op jit(solution)/shard_map/all_to_all | solution.py:514
  78.8 2.4 %fusion.last_tiles_ref.tiles_ref = s32[128]{0:T(128)S(1)} fusion(bf16[128,40,128]{2,1,0:T(8,128)(2,1)S(1)} %all-to-all-done.1.last_ref.arrived_ref), kind=kLoop, calls=%fused_computation.1 | loop fusion | flops 128 | bytes 768 | tf_op jit(solution)/shard_map/convert_element_type | solution.py:510
  81.2 0.0 copy-start.4
  81.2 1.6 copy-done.4
  82.8 20.6 %grid_step.1 = (f32[3,32,4096]{2,1,0:T(8,128)}, bf16[32,48,256]{2,1,0:T(8,128)(2,1)S(1)}, bf16[128,24,128]{2,1,0:T(8,128)(2,1)}) custom-call(s32[128]{0:T(128)S(1)} %fusion.last_tiles_ref.tiles_ref, bf16[128,40,128]{2,1,0:T(8,128)(2,1)S(1)} %all-to-all-done.1.last_ref.arrived_ref, s32[128]{0:T(128)S(1)} %convert_reduce_fusion.tiles_ref, ...), custom_call_target="tpu_custom_call" | custom-call | flops 10000000000 | bytes 4194304 | tf_op jit(solution)/shard_map/grid_step/pallas_call | solution.py:433
  103.5 0.0 copy-start.5
  103.5 0.9 copy-done.5
  104.4 21.1 %all-to-all-start.2 = ((bf16[128,24,128]{2,1,0:T(8,128)(2,1)}), bf16[128,24,128]{2,1,0:T(8,128)(2,1)S(1)}, u32[]{:S(2)}, u32[]{:S(2)}) async-start(bf16[128,24,128]{2,1,0:T(8,128)(2,1)} %get-tuple-element.19), calls=%async_computation.2 | async-start | bytes 1572864 | tf_op jit(solution)/shard_map/all_to_all | solution.py:514
  125.5 0.0 copy-start.6
  125.5 1.1 copy-done.6
  126.6 4.1 %gather_step.1 = bf16[128,24,128]{2,1,0:T(8,128)(2,1)S(1)} custom-call(s32[128]{0:T(128)S(1)} %fusion.last_tiles_ref.tiles_ref, bf16[128,40,128]{2,1,0:T(8,128)(2,1)S(1)} %all-to-all-done.1.last_ref.arrived_ref, bf16[32,48,256]{2,1,0:T(8,128)(2,1)S(1)} %copy-done.6), custom_call_target="tpu_custom_call" | custom-call | flops 10000000000 | bytes 4194304 | tf_op jit(solution)/shard_map/gather_step/pallas_call | solution.py:451
  130.7 0.0 copy-start.1
  130.7 0.0 copy-start.2
  130.8 13.4 %all-to-all-done.2.refs_0_ = bf16[128,24,128]{2,1,0:T(8,128)(2,1)S(1)} async-done(((bf16[128,24,128]{2,1,0:T(8,128)(2,1)}), bf16[128,24,128]{2,1,0:T(8,128)(2,1)S(1)}, u32[]{:S(2)}, u32[]{:S(2)}) %all-to-all-start.2) | async-done | bytes 786464 | tf_op jit(solution)/shard_map/all_to_all | solution.py:514
  144.1 25.3 %all_to_all.21.refs_1_ = bf16[128,24,128]{2,1,0:T(8,128)(2,1)S(1)} all-to-all(bf16[128,24,128]{2,1,0:T(8,128)(2,1)S(1)} %gather_step.1), channel_id=1, replica_groups=mesh['gx'=2,'gy'=4,'gz'=4] {'gy','gz'}, dimensions={0} | all-to-all | bytes 1572864 | tf_op jit(solution)/shard_map/all_to_all | solution.py:514
  169.4 0.0 copy-done.1
  169.4 0.0 copy-done.2
  169.4 3.9 %unpack.1 = (f32[3,32768]{1,0:T(4,128)}, f32[9,32768]{1,0:T(8,128)}) custom-call(s32[64]{0:T(128)S(1)} %copy-done.2, s32[64]{0:T(128)S(1)} %copy-done.1, bf16[128,24,128]{2,1,0:T(8,128)(2,1)S(1)} %all-to-all-done.2.refs_0_, bf16[128,24,128]{2,1,0:T(8,128)(2,1)S(1)} %all_to_all.21.refs_1_), custom_call_target="tpu_custom_call" | custom-call | tf_op jit(solution)/shard_map/unpack/pallas_call | solution.py:496
Async XLA Ops:
  47.4 4.2 %copy-start = (f32[32,4096]{1,0:T(8,128)S(1)}, f32[32,4096]{1,0:T(8,128)}, u32[]{:S(2)}) copy-start(f32[32,4096]{1,0:T(8,128)} %drag_ref.1) | copy-start | bytes 1572868
  47.4 31.4 %all-to-all-start.1 = ((bf16[128,40,128]{2,1,0:T(8,128)(2,1)}), bf16[128,40,128]{2,1,0:T(8,128)(2,1)S(1)}, u32[]{:S(2)}, u32[]{:S(2)}) async-start(bf16[128,40,128]{2,1,0:T(8,128)(2,1)} %get-tuple-element.15), calls=%async_computation.1 | async-start | bytes 2621440 | tf_op jit(solution)/shard_map/all_to_all | solution.py:514
  73.0 1.4 copy-start.3
  81.2 1.6 copy-start.4
  103.5 0.9 copy-start.5
  104.4 39.8 %all-to-all-start.2 = ((bf16[128,24,128]{2,1,0:T(8,128)(2,1)}), bf16[128,24,128]{2,1,0:T(8,128)(2,1)S(1)}, u32[]{:S(2)}, u32[]{:S(2)}) async-start(bf16[128,24,128]{2,1,0:T(8,128)(2,1)} %get-tuple-element.19), calls=%async_computation.2 | async-start | bytes 1572864 | tf_op jit(solution)/shard_map/all_to_all | solution.py:514
  125.5 1.1 copy-start.6
  130.7 38.7 %copy-start.1 = (s32[64]{0:T(128)S(1)}, s32[64]{0:T(128)}, u32[]{:S(2)}) copy-start(s32[64]{0:T(128)} %count_ref.3) | copy-start | bytes 772
  130.7 38.7 %copy-start.2 = (s32[64]{0:T(128)S(1)}, s32[64]{0:T(128)}, u32[]{:S(2)}) copy-start(s32[64]{0:T(128)} %get-tuple-element.18.dest_ref) | copy-start | bytes 772
where the time goes:
time: 175 us; the launch traced here: 173 us
  blocking collectives  64.1 us (37%)
  Pallas kernels  54.2 us (31%)
  starting transfers between devices  25.3 us (14%)
  waiting for transfers between devices  17.8 us (10%)
  local copies, waits for them, and re-layouts  6.57 us (4%)
  other arithmetic  4.71 us (3%)
    all_to_all x2, blocking collectives, exchange(): lax.all_to_all(value, GROUP_AXES, split_axis=0, concat_axis=0, tiled=True)  64.1 us
    all_to_all x2, starting transfers between devices, exchange(): lax.all_to_all(value, GROUP_AXES, split_axis=0, concat_axis=0, tiled=True)  25.3 us
    pallas_call x1, Pallas kernels, grid_step(): pl.pallas_call(grid_kernel, name='grid_step', out_shape=(jax.ShapeDtypeSt...  20.6 us
    pallas_call x1, Pallas kernels, scatter_step(): pl.pallas_call(scatter_kernel, name='scatter_step', out_shape=jax.ShapeDt...  18.6 us
    all_to_all x2, waiting for transfers between devices, exchange(): lax.all_to_all(value, GROUP_AXES, split_axis=0, concat_axis=0, tiled=True)  17.8 us
    pallas_call x1, Pallas kernels, pack(): pl.pallas_call(functools.partial(pack_kernel, portion), name='pack', out_...  6.42 us
    unnamed x14, local copies, waits for them, and re-layouts  4.99 us
    convert_element_type x2, other arithmetic, tile_marks(): return arrived[:, FIELDS - 1, 0].astype(jnp.int32)  4.71 us
  transfers between devices with their start and end apart: 2, of which 2 were waited for; matrix products, arithmetic and copies ran while one was open for 1% of the time, Pallas kernels for 13%

commit v1 on v0

v1 whole, which is shorter than its diff:
```python
import functools

import jax
import jax.numpy as jnp
from jax import lax
from jax.experimental import pallas as pl
from jax.experimental.pallas import tpu as pltpu
from jax.sharding import PartitionSpec as P

EDGE = 16
QUANT = 1024
LANES = 128
FIELDS = 16
RESULTS = 12
PARTS = 4
GROUP_AXES = ("gy", "gz")
F32 = jnp.float32
BF16 = jnp.bfloat16
MESH = pl.DeviceIdType.MESH


SMEM = pl.BlockSpec(memory_space=pltpu.SMEM)
VMEM = pl.BlockSpec(memory_space=pltpu.VMEM)
HBM = pl.BlockSpec(memory_space=pltpu.HBM)


def cost(flops):
    return pl.CostEstimate(flops=flops, bytes_accessed=1 << 22, transcendentals=0)


def plan_kernel(
    cap, owner_ref, slot_ref, count_ref, table_ref, live_ref, dest_ref, marks_ref, used_ref, tile_ref
):
    group = used_ref.shape[0]

    def clear_used(i, carry):
        used_ref[i] = 0
        return carry

    def clear_slots(i, carry):
        table_ref[i] = 0
        live_ref[i] = 0
        tile_ref[i] = -1
        return carry

    lax.fori_loop(0, group, clear_used, 0)
    lax.fori_loop(0, group * cap, clear_slots, 0, unroll=8)

    def place(block, carry):
        owner = owner_ref[block]
        rank = used_ref[owner]
        used_ref[owner] = rank + 1
        where = owner * cap + rank
        table_ref[where] = block
        live_ref[where] = count_ref[block]
        tile_ref[where] = slot_ref[block]
        dest_ref[block] = where
        return carry

    lax.fori_loop(0, owner_ref.shape[0], place, 0)
    lane = lax.broadcasted_iota(jnp.int32, (1, LANES), 1)

    def mark(owner, carry):
        row = jnp.full((1, LANES), -1, jnp.int32)
        for i in range(cap):
            row = jnp.where(lane == i, tile_ref[owner * cap + i], row)
        marks_ref[owner] = row
        return carry

    lax.fori_loop(0, group, mark, 0)


def plan(cap, group, owner, slot, count):
    slots = group * cap
    return pl.pallas_call(
        functools.partial(plan_kernel, cap),
        name="plan",
        out_shape=(
            jax.ShapeDtypeStruct((slots,), jnp.int32),
            jax.ShapeDtypeStruct((slots,), jnp.int32),
            jax.ShapeDtypeStruct(owner.shape, jnp.int32),
            jax.ShapeDtypeStruct((group, 1, LANES), jnp.int32),
        ),
        in_specs=[SMEM] * 3,
        out_specs=(SMEM, SMEM, SMEM, VMEM),
        scratch_shapes=[pltpu.SMEM((group,), jnp.int32), pltpu.SMEM((slots,), jnp.int32)],
    )(owner, slot, count)


class Group:
    def __init__(self):
        self.wide = lax.axis_size(GROUP_AXES[1])
        self.size = lax.axis_size(GROUP_AXES)
        self.me = lax.axis_index(GROUP_AXES[0]) * self.wide + lax.axis_index(GROUP_AXES[1])

    def device(self, peer):
        return {GROUP_AXES[0]: peer // self.wide, GROUP_AXES[1]: peer % self.wide}

    def greet(self):
        barrier = pltpu.get_barrier_semaphore()

        def signal(k, carry):
            pl.semaphore_signal(
                barrier, inc=1, device_id=self.device(self.me ^ k), device_id_type=MESH
            )
            return carry

        lax.fori_loop(1, self.size, signal, 0)

    def gathered(self):
        pl.semaphore_wait(pltpu.get_barrier_semaphore(), self.size - 1)


def twice(rows):
    return jnp.concatenate([rows, rows], axis=0)


def span_of(part):
    return slice(part * LANES, (part + 1) * LANES)


def encode(code):
    power = code >> 8
    scale = jnp.where(
        power < 28,
        (1 << (power & 31)).astype(F32),
        (1 << jnp.maximum(power - 28, 0)).astype(F32) * 2.0**28,
    )
    size = ((code & 127) + 128).astype(F32) * (scale * 2.0**-28)
    return jnp.where((code & 128) != 0, -size, size)


def decode(value):
    size = jnp.abs(value)
    position = jnp.where(value < 0.0, 128.0 / QUANT, 0.0)
    for bit in (32, 16, 8, 4, 2, 1):
        large = size >= 2.0 ** (7 + bit - 28)
        size = jnp.where(large, size * 2.0**-bit, size)
        position = jnp.where(large, position + bit * 256.0 / QUANT, position)
    return position + (size * (2.0**28 / QUANT) + (0.5 + 0.5 / QUANT - 128.0 / QUANT))


def load_item(u, item_ref, fields_ref):
    rows = item_ref.shape[0]
    first = u * rows
    fields_ref[first : first + rows] = item_ref[...].astype(F32)
    for q in range(rows // FIELDS):
        base = first + q * FIELDS
        fields_ref[base + 13 : base + 16] = decode(fields_ref[base + 13 : base + 16])

    def spread(field, part):
        return twice(
            jnp.concatenate(
                [
                    jnp.broadcast_to(fields_ref[pl.ds(row, 1), :], (8, LANES))
                    for row in (
                        first + (part * 2) * FIELDS + field,
                        first + (part * 2 + 1) * FIELDS + field,
                    )
                ],
                axis=1,
            )
        )

    return spread


def stencil(position, node):
    offset = node - position
    magnitude = jnp.abs(offset)
    outer_part = jnp.maximum(1.5 - magnitude, 0.0)
    weight = jnp.where(
        magnitude < 0.5, 0.75 - magnitude * magnitude, 0.5 * outer_part * outer_part
    )
    return weight, weight * offset


def planes(u, spread, part, node, rows_ref):
    factors_y = stencil(spread(14, part), node)
    factors_z = [factor.astype(BF16) for factor in stencil(spread(15, part), node)]
    firsts = [((u * 2 + part) * 2 + k) * 2 * EDGE for k in range(2)]
    for first, factor in zip(firsts, factors_y):
        for q in range(2):
            rows_ref[first + q * EDGE : first + (q + 1) * EDGE] = factor[:, span_of(q)]

    def row(first, y):
        return jnp.concatenate(
            [
                twice(
                    jnp.broadcast_to(rows_ref[pl.ds(first + q * EDGE + y, 1), :], (8, LANES))
                ).astype(BF16)
                for q in range(2)
            ],
            axis=1,
        )

    zero, one, two = [], [], []
    for y in range(EDGE):
        weight_row, slope_row = row(firsts[0], y), row(firsts[1], y)
        zero.append(weight_row * factors_z[0])
        one.append(slope_row * factors_z[0])
        two.append(weight_row * factors_z[1])
    return [jnp.concatenate(parts, axis=0) for parts in (zero, one, two)]


def nodes():
    return lax.broadcasted_iota(jnp.int32, (EDGE, 2 * LANES), 0).astype(F32)


def deposit(u, item_ref, fields_ref, rows_ref):
    spread = load_item(u, item_ref, fields_ref)
    node = nodes()
    total = None
    for part in range(item_ref.shape[0] // (2 * FIELDS)):
        weight_x, slope_x = stencil(spread(13, part), node)
        mass = spread(0, part)
        mass_x = mass * weight_x
        mass_slope = mass * slope_x
        nothing = jnp.zeros(mass_x.shape, BF16)
        lead_zero, lead_one, lead_two = [mass_x.astype(BF16)], [nothing], [nothing]
        for d in range(3):
            lead_zero.append(
                (spread(1 + d, part) * mass_x + spread(4 + 3 * d, part) * mass_slope).astype(BF16)
            )
            lead_one.append((spread(5 + 3 * d, part) * mass_x).astype(BF16))
            lead_two.append((spread(6 + 3 * d, part) * mass_x).astype(BF16))
        lead = jnp.concatenate(
            [jnp.concatenate(rows, axis=0) for rows in (lead_zero, lead_one, lead_two)], axis=1
        )
        plane = jnp.concatenate(planes(u, spread, part, node, rows_ref), axis=1)
        sums = lax.dot_general(
            lead, plane, (((1,), (1,)), ((), ())), preferred_element_type=F32
        )
        total = sums if total is None else total + sums
    return total


def interpolate(u, item_ref, grid_rows, fields_ref, rows_ref, parts_ref):
    spread = load_item(u, item_ref, fields_ref)
    node = nodes()
    quarters = item_ref.shape[0] // FIELDS
    first = u * quarters * RESULTS * 8
    for part in range(quarters // 2):
        weight_x, slope_x = stencil(spread(13, part), node)
        moments = [
            jnp.dot(grid_rows, plane, preferred_element_type=F32)
            for plane in planes(u, spread, part, node, rows_ref)
        ]
        slope_four = 4.0 * slope_x
        weight_four = 4.0 * weight_x
        for d in range(3):
            span = slice(d * EDGE, (d + 1) * EDGE)
            entries = (
                (d, weight_x, moments[0]),
                (3 + 3 * d, slope_four, moments[0]),
                (4 + 3 * d, weight_four, moments[1]),
                (5 + 3 * d, weight_four, moments[2]),
            )
            for entry, factor, moment in entries:
                product = factor * moment[span]
                partial = product[:8] + product[8:]
                for q in range(2):
                    at = first + ((part * 2 + q) * RESULTS + entry) * 8
                    parts_ref[at : at + 8] = partial[:, span_of(q)]
    groups = []
    for g in range(quarters * RESULTS // 8):
        total = parts_ref[pl.ds(first + g * 64, 8, stride=8), :]
        for j in range(1, 8):
            total = total + parts_ref[pl.ds(first + g * 64 + j, 8, stride=8), :]
        groups.append(total)
    return jnp.concatenate(groups, axis=0).astype(BF16)


def scatter_kernel(
    cap,
    subs,
    table_ref,
    live_ref,
    marks_ref,
    mass_ref,
    velocity_ref,
    affine_ref,
    cell_ref,
    fraction_ref,
    arrived_ref,
    sums_ref,
    told_ref,
    mass_v,
    velocity_v,
    affine_v,
    cell_v,
    fraction_v,
    stage_ref,
    packed_ref,
    fields_ref,
    rows_ref,
    load_sems,
    send_sems,
    recv_sems,
    mark_send,
    mark_recv,
):
    group = Group()
    n, me = group.size, group.me
    per = cap // subs
    blocks, _, width = mass_v.shape
    quarters = width // LANES
    sources = (velocity_ref, affine_ref, cell_ref, fraction_ref)
    staged = (velocity_v, affine_v, cell_v, fraction_v)
    mass_load = pltpu.make_async_copy(mass_ref, mass_v, load_sems.at[len(sources)])
    mass_load.start()

    def load_block(block, carry):
        cols = pl.ds(pl.multiple_of(block * width, LANES), width)
        for i, (source, target) in enumerate(zip(sources, staged)):
            pltpu.make_async_copy(
                source.at[:, cols], target.at[block], load_sems.at[i]
            ).start()
        return carry

    lax.fori_loop(0, blocks, load_block, 0, unroll=4)
    group.greet()
    lane = lax.broadcasted_iota(jnp.int32, (1, width), 1)
    mass_load.wait()
    for i, target in enumerate(staged):
        pltpu.make_async_copy(target, target, load_sems.at[i]).wait()

    def pack(slot):
        block = table_ref[slot]
        live = jnp.where(lane < live_ref[slot], mass_v[block], 0.0)
        velocity = velocity_v[block]
        affine = affine_v[block]
        code = encode(cell_v[block] * QUANT + fraction_v[block])
        for q in range(quarters):
            base = q * FIELDS
            stage_ref[base : base + 1] = live[:, span_of(q)]
            stage_ref[base + 1 : base + 4] = velocity[:, span_of(q)]
            stage_ref[base + 4 : base + 13] = affine[:, span_of(q)]
            stage_ref[base + 13 : base + 16] = code[:, span_of(q)]
        packed_ref[slot] = stage_ref[...].astype(BF16)

    def rows_of(device, sub):
        return pl.ds(device * cap + sub * per, per)

    def transfer(k, sub):
        peer = me ^ k
        return pltpu.make_async_remote_copy(
            src_ref=packed_ref.at[rows_of(peer, sub)],
            dst_ref=arrived_ref.at[rows_of(me, sub)],
            send_sem=send_sems.at[k, sub],
            recv_sem=recv_sems.at[k, sub],
            device_id=group.device(peer),
            device_id_type=MESH,
        )

    def arrival(k, sub):
        rows = rows_of(me ^ k, sub)
        return pltpu.make_async_copy(
            packed_ref.at[rows], arrived_ref.at[rows], recv_sems.at[k, sub]
        )

    def mark_transfer(k):
        peer = me ^ k
        return pltpu.make_async_remote_copy(
            src_ref=marks_ref.at[peer],
            dst_ref=told_ref.at[me],
            send_sem=mark_send.at[k],
            recv_sem=mark_recv.at[k],
            device_id=group.device(peer),
            device_id_type=MESH,
        )

    own_marks = pltpu.make_async_copy(marks_ref.at[me], told_ref.at[me], mark_recv.at[0])
    own_marks.start()

    def pack_step(step):
        k = n - 1 - step % n
        sub = step // n
        for i in range(per):
            pack((me ^ k) * cap + sub * per + i)

    def send_step(step):
        k = n - 1 - step % n
        sub = step // n

        @pl.when(k != 0)
        def _():
            transfer(k, sub).start()

        @pl.when(k == 0)
        def _():
            arrival(0, sub).start()

    pack_step(0)
    group.gathered()

    def pack_and_send(step, carry):
        pack_step(step)
        send_step(step - 1)
        return carry

    lax.fori_loop(1, n * subs, pack_and_send, 0)

    def send_marks(k, carry):
        mark_transfer(k).start()
        return carry

    lax.fori_loop(1, n, send_marks, 0)
    send_step(n * subs - 1)

    pair = 2

    def take(step, carry):
        sub = step // (n // pair)
        first = (step % (n // pair)) * pair
        for j in range(pair):
            arrival(first + j, sub).wait()
        for j in range(pair):
            for i in range(per):
                slot = (me ^ (first + j)) * cap + sub * per + i
                sums_ref[slot] = deposit(
                    j * per + i, arrived_ref.at[slot], fields_ref, rows_ref
                )
        return carry

    lax.fori_loop(0, n // pair * subs, take, 0)
    own_marks.wait()

    def settle(k, carry):
        mark_transfer(k).wait_recv()
        mark_transfer(k).wait_send()
        for sub in range(subs):
            transfer(k, sub).wait_send()
        return carry

    lax.fori_loop(1, n, settle, 0)


def scatter(cap, subs, group, table, live, marks, mass, velocity, affine, cell, fraction):
    slots = group * cap
    blocks, _, width = mass.shape
    quarters = width // LANES
    rows = quarters * FIELDS
    unroll = 2 * (cap // subs)
    arrays = (mass, velocity, affine, cell, fraction)
    return pl.pallas_call(
        functools.partial(scatter_kernel, cap, subs),
        name="scatter_step",
        out_shape=(
            jax.ShapeDtypeStruct((slots, rows, LANES), BF16),
            jax.ShapeDtypeStruct((slots, 4 * EDGE, EDGE * EDGE), F32),
            jax.ShapeDtypeStruct(marks.shape, jnp.int32),
        ),
        in_specs=[SMEM, SMEM, VMEM] + [HBM] * 5,
        out_specs=(VMEM,) * 3,
        scratch_shapes=[pltpu.VMEM(mass.shape, F32)]
        + [
            pltpu.VMEM((blocks, array.shape[0], width), array.dtype) for array in arrays[1:]
        ]
        + [
            pltpu.VMEM((rows, LANES), F32),
            pltpu.VMEM((slots, rows, LANES), BF16),
            pltpu.VMEM((unroll * rows, LANES), F32),
            pltpu.VMEM((unroll * 2 * quarters * EDGE, LANES), F32),
            pltpu.SemaphoreType.DMA((len(arrays),)),
            pltpu.SemaphoreType.DMA((group, subs)),
            pltpu.SemaphoreType.DMA((group, subs)),
            pltpu.SemaphoreType.DMA((group,)),
            pltpu.SemaphoreType.DMA((group,)),
        ],
        compiler_params=pltpu.CompilerParams(
            collective_id=0, has_side_effects=True, vmem_limit_bytes=40 << 20
        ),
        cost_estimate=cost(10**10),
    )(table, live, marks, *arrays)


def grid_kernel(cap, told_ref, deposits_ref, drag_ref, grid_ref, round_ref, sums_ref):
    plane_size = EDGE * EDGE

    def start(t, carry):
        for x in range(EDGE):
            sums_ref[t, x : x + 1, :] = drag_ref[
                pl.ds(t, 1), x * plane_size : (x + 1) * plane_size
            ]
        sums_ref[t, EDGE:, :] = jnp.zeros((3 * EDGE, plane_size), F32)
        return carry

    lax.fori_loop(0, drag_ref.shape[0], start, 0)

    def add(device, carry):
        for i in range(cap):
            tile = told_ref[device, 0, i]

            @pl.when(tile >= 0)
            def _():
                sums_ref[tile] += deposits_ref[device * cap + i]

        return carry

    lax.fori_loop(0, told_ref.shape[0], add, 0)

    def divide(t, carry):
        mass = sums_ref[t, :EDGE, :]
        parts = [sums_ref[t, (d + 1) * EDGE : (d + 2) * EDGE, :] / mass for d in range(3)]
        round_ref[t] = jnp.concatenate(parts, axis=0).astype(BF16)
        for d in range(3):
            for x in range(EDGE):
                grid_ref[d, pl.ds(t, 1), x * plane_size : (x + 1) * plane_size] = parts[d][
                    x : x + 1
                ]
        return carry

    lax.fori_loop(0, round_ref.shape[0], divide, 0)


def grid_step(cap, told, deposits, drag):
    tiles = drag.shape[0]
    plane_size = EDGE * EDGE
    return pl.pallas_call(
        functools.partial(grid_kernel, cap),
        name="grid_step",
        out_shape=(
            jax.ShapeDtypeStruct((3, tiles, EDGE * plane_size), F32),
            jax.ShapeDtypeStruct((tiles, 3 * EDGE, plane_size), BF16),
        ),
        in_specs=[SMEM, VMEM, VMEM],
        out_specs=(VMEM, VMEM),
        scratch_shapes=[pltpu.VMEM((tiles, 4 * EDGE, plane_size), F32)],
        compiler_params=pltpu.CompilerParams(vmem_limit_bytes=20 << 20),
        cost_estimate=cost(10**9),
    )(told, deposits, drag)


def gather_kernel(
    cap,
    subs,
    told_ref,
    arrived_ref,
    round_ref,
    returned_ref,
    results_ref,
    fields_ref,
    rows_ref,
    parts_ref,
    send_sems,
    recv_sems,
):
    group = Group()
    n, me = group.size, group.me
    per = cap // subs
    group.greet()

    def rows_of(device, sub):
        return pl.ds(device * cap + sub * per, per)

    def transfer(k, sub):
        peer = me ^ k
        return pltpu.make_async_remote_copy(
            src_ref=results_ref.at[rows_of(peer, sub)],
            dst_ref=returned_ref.at[rows_of(me, sub)],
            send_sem=send_sems.at[k, sub],
            recv_sem=recv_sems.at[k, sub],
            device_id=group.device(peer),
            device_id_type=MESH,
        )

    def arrival(k, sub):
        rows = rows_of(me ^ k, sub)
        return pltpu.make_async_copy(
            results_ref.at[rows], returned_ref.at[rows], recv_sems.at[k, sub]
        )

    pair = 2
    half = n // 2
    strides = half // pair

    def place(step):
        side = step // (strides * subs)
        rest = step % (strides * subs)
        return n - 1 - side * half - (rest % strides) * pair, rest // strides

    def work(step):
        top, sub = place(step)
        for j in range(pair):
            source = me ^ (top - j)
            for i in range(per):
                slot = source * cap + sub * per + i
                tile = jnp.maximum(told_ref[source, 0, sub * per + i], 0)
                results_ref[slot] = interpolate(
                    j * per + i,
                    arrived_ref.at[slot],
                    round_ref[tile],
                    fields_ref,
                    rows_ref,
                    parts_ref,
                )

    def send(step):
        top, sub = place(step)
        for j in range(pair):
            k = top - j

            @pl.when(k != 0)
            def _():
                transfer(k, sub).start()

            @pl.when(k == 0)
            def _():
                arrival(0, sub).start()

    steps = half // pair * subs * 2
    work(0)
    group.gathered()

    def work_and_send(step, carry):
        work(step)
        send(step - 1)
        return carry

    lax.fori_loop(1, steps, work_and_send, 0)
    send(steps - 1)

    def settle(k, carry):
        for sub in range(subs):
            transfer(k, sub).wait_recv()
            transfer(k, sub).wait_send()
        return carry

    for sub in range(subs):
        arrival(0, sub).wait()
    lax.fori_loop(1, n, settle, 0)


def gather(cap, subs, told, arrived, rounded):
    slots, rows, _ = arrived.shape
    group = told.shape[0]
    quarters = rows // FIELDS
    unroll = 2 * (cap // subs)
    result = (slots, quarters * RESULTS, LANES)
    return pl.pallas_call(
        functools.partial(gather_kernel, cap, subs),
        name="gather_step",
        out_shape=jax.ShapeDtypeStruct(result, BF16),
        in_specs=[SMEM, VMEM, VMEM],
        out_specs=VMEM,
        scratch_shapes=[
            pltpu.VMEM(result, BF16),
            pltpu.VMEM((unroll * rows, LANES), F32),
            pltpu.VMEM((unroll * 2 * quarters * EDGE, LANES), F32),
            pltpu.VMEM((unroll * quarters * RESULTS * 8, LANES), F32),
            pltpu.SemaphoreType.DMA((group, subs)),
            pltpu.SemaphoreType.DMA((group, subs)),
        ],
        compiler_params=pltpu.CompilerParams(
            collective_id=1, has_side_effects=True, vmem_limit_bytes=40 << 20
        ),
        cost_estimate=cost(10**10),
    )(told, arrived, rounded)


def unpack_kernel(dest_ref, count_ref, returned_ref, velocity_ref, affine_ref):
    blocks = dest_ref.shape[0]
    width = velocity_ref.shape[1] // blocks
    lane = lax.broadcasted_iota(jnp.int32, (1, LANES), 1)

    def unpack(block, carry):
        count = count_ref[block]
        rows = returned_ref[dest_ref[block]].astype(F32)
        for q in range(width // LANES):
            first = q * LANES
            cols = pl.ds(pl.multiple_of(block * width + first, LANES), LANES)
            part = jnp.where(lane + first < count, rows[q * RESULTS : (q + 1) * RESULTS], 0.0)
            velocity_ref[:, cols] = part[:3]
            affine_ref[:, cols] = part[3:]
        return carry

    lax.fori_loop(0, blocks, unpack, 0)


def unpack(dest, count, returned, width):
    particles = dest.shape[0] * width
    return pl.pallas_call(
        unpack_kernel,
        name="unpack",
        out_shape=(
            jax.ShapeDtypeStruct((3, particles), F32),
            jax.ShapeDtypeStruct((9, particles), F32),
        ),
        in_specs=[SMEM, SMEM, VMEM],
        out_specs=(VMEM, VMEM),
        compiler_params=pltpu.CompilerParams(vmem_limit_bytes=20 << 20),
    )(dest, count, returned)


def per_device(
    particle_mass,
    particle_velocity,
    particle_affine,
    particle_cell,
    particle_fraction,
    block_owner,
    block_slot,
    block_count,
    cell_drag,
):
    group = lax.axis_size(GROUP_AXES)
    blocks = block_count.shape[0]
    width = particle_mass.shape[0] // blocks
    cap = max(1, 2 * blocks // group)
    subs = min(cap, PARTS)
    table, live, dest, marks = plan(cap, group, block_owner[:, 0], block_slot, block_count)
    arrived, deposits, told = scatter(
        cap,
        subs,
        group,
        table,
        live,
        marks,
        particle_mass.reshape(blocks, 1, width),
        particle_velocity,
        particle_affine,
        particle_cell,
        particle_fraction,
    )
    grid_velocity, rounded = grid_step(cap, told, deposits, cell_drag)
    returned = gather(cap, subs, told, arrived, rounded)
    new_velocity, new_affine = unpack(dest, block_count, returned, width)
    return jnp.transpose(grid_velocity, (1, 0, 2)), new_velocity, new_affine


def solution(mesh):
    everywhere = ("gx", "gy", "gz")
    return jax.shard_map(
        per_device,
        mesh=mesh,
        in_specs=(
            P(everywhere),
            P(None, everywhere),
            P(None, everywhere),
            P(None, everywhere),
            P(None, everywhere),
            P(everywhere, None),
            P(everywhere),
            P(everywhere),
            P(everywhere, None),
        ),
        out_specs=(P(everywhere, None, None), P(None, everywhere), P(None, everywhere)),
        check_vma=False,
    )
```

time: 175 us -> 131 us (0.75)
  Pallas kernels: 54.2 us -> 122 us
  blocking collectives: 64.1 us -> 0 us
  starting transfers between devices: 25.3 us -> 0 us
  waiting for transfers between devices: 17.8 us -> 0 us
  other arithmetic: 4.71 us -> 0 us
    pallas_call x5 -> x4, Pallas kernels: 50.3 us -> 119 us  [the longest x1 70.4 us: scatter(): pl.pallas_call(functools.partial(scatter_kernel, cap, subs), name='scatte...]
    all_to_all x2 -> x0, blocking collectives: 64.1 us -> none  [exchange(): lax.all_to_all(value, GROUP_AXES, split_axis=0, concat_axis=0, tiled=True)]
    all_to_all x2 -> x0, starting transfers between devices: 25.3 us -> none  [exchange(): lax.all_to_all(value, GROUP_AXES, split_axis=0, concat_axis=0, tiled=True)]
    all_to_all x2 -> x0, waiting for transfers between devices: 17.8 us -> none  [exchange(): lax.all_to_all(value, GROUP_AXES, split_axis=0, concat_axis=0, tiled=True)]
    convert_element_type x2 -> x0, other arithmetic: 4.71 us -> none  [tile_marks(): return arrived[:, FIELDS - 1, 0].astype(jnp.int32)]
    unnamed x14 -> x22, local copies, waits for them, and re-layouts: 4.99 us -> 7.63 us
  transfers between devices with their start and end apart: 2 -> 0, of which waited for: 2 -> 0; matrix products, arithmetic and copies ran while one was open for 1% -> 0% of each run, Pallas kernels for 13% -> 0%
where the time goes in v1:
time: 131 us
  Pallas kernels  122 us (93%)
  local copies, waits for them, and re-layouts  7.63 us (6%)
    pallas_call x1, Pallas kernels, scatter(): pl.pallas_call(functools.partial(scatter_kernel, cap, subs), name='scatte...  70.4 us
    pallas_call x1, Pallas kernels, gather(): pl.pallas_call(functools.partial(gather_kernel, cap, subs), name='gather_...  41.5 us
    unnamed x22, local copies, waits for them, and re-layouts  7.63 us
    pallas_call x1, Pallas kernels, grid_step(): pl.pallas_call(functools.partial(grid_kernel, cap), name='grid_step', out...  4.78 us
    pallas_call x1, Pallas kernels, unpack(): pl.pallas_call(unpack_kernel, name='unpack', out_shape=(jax.ShapeDtypeStr...  2.88 us
    pallas_call x1, Pallas kernels, plan(): pl.pallas_call(functools.partial(plan_kernel, cap), name='plan', out_shap...  2.74 us

profile of v1, /device:TPU:0, one launch (start us, length us, event | category | flops | bytes accessed | tf_op | source)
XLA Modules:
  0.0 130.6 jit_solution(12264079573762086630)
XLA Ops:
  0.6 2.7 %plan.1 = (s32[128]{0:T(128)}, s32[128]{0:T(128)}, s32[64]{0:T(128)}, s32[16,1,128]{2,1,0:T(1,128)}) custom-call(s32[64]{0:T(128)} %bitcast.5, s32[64]{0:T(128)} %slot_ref.1, s32[64]{0:T(128)} %count_ref.3), custom_call_target="tpu_custom_call" | custom-call | tf_op jit(solution)/shard_map/plan/pallas_call | solution.py:75
  3.4 0.0 copy-start.3
  3.4 1.6 %copy-done.3 = f32[9,32768]{1,0:T(8,128)S(1)} copy-done((f32[9,32768]{1,0:T(8,128)S(1)}, f32[9,32768]{1,0:T(8,128)}, u32[]{:S(2)}) %copy-start.3) | copy-done | bytes 1179672
  5.0 0.0 copy-start.4
  5.0 1.0 copy-done.4
  6.0 0.0 copy-start.5
  6.0 1.0 copy-done.5
  7.1 0.0 copy-start.6
  7.1 1.0 copy-done.6
  8.1 0.0 copy-start.7
  8.1 0.9 copy-done.7
  9.0 0.0 copy-start.8
  9.0 0.7 copy-done.8
  9.7 0.0 copy-start.9
  9.7 0.7 copy-done.9
  10.4 0.0 copy-start.10
  10.4 0.7 copy-done.10
  11.0 0.0 copy-start
  11.0 70.4 %scatter_step.1 = (bf16[128,64,128]{2,1,0:T(8,128)(2,1)S(1)}, f32[128,64,256]{2,1,0:T(8,128)S(1)}, s32[16,1,128]{2,1,0:T(1,128)S(1)}) custom-call(s32[128]{0:T(128)S(1)} %copy-done.9, s32[128]{0:T(128)S(1)} %copy-done.10, s32[16,1,128]{2,1,0:T(1,128)S(1)} %copy-done.8, f32[64,1,512]{2,1,0:T(1,128)S(1)} %bitcast.3, f32[3,32768]{1,0:T(4,128)S(1)} %copy-done.4, ...), custom_call_target="tpu_custom_call" | custom-call | flops 10000000000 | bytes 4194304 | tf_op jit(solution)/shard_map/scatter_step/pallas_call | solution.py:446
  81.5 0.0 copy-done
  81.5 4.8 %grid_step.1 = (f32[3,32,4096]{2,1,0:T(8,128)}, bf16[32,48,256]{2,1,0:T(8,128)(2,1)S(1)}) custom-call(s32[16,1,128]{2,1,0:T(1,128)S(1)} %get-tuple-element.17.told_ref, f32[128,64,256]{2,1,0:T(8,128)S(1)} %get-tuple-element.18.deposits_ref, f32[32,4096]{1,0:T(8,128)S(1)} %copy-done), custom_call_target="tpu_custom_call" | custom-call | flops 1000000000 | bytes 4194304 | tf_op jit(solution)/shard_map/grid_step/pallas_call | solution.py:520
  86.2 0.0 copy-start.1
  86.2 0.0 copy-start.2
  86.3 41.5 %gather_step.1.returned_ref = bf16[128,48,128]{2,1,0:T(8,128)(2,1)S(1)} custom-call(s32[16,1,128]{2,1,0:T(1,128)S(1)} %get-tuple-element.17.told_ref, bf16[128,64,128]{2,1,0:T(8,128)(2,1)S(1)} %get-tuple-element.21.arrived_ref, bf16[32,48,256]{2,1,0:T(8,128)(2,1)S(1)} %get-tuple-element.22.round_ref), custom_call_target="tpu_custom_call" | custom-call | flops 10000000000 | bytes 4194304 | tf_op jit(solution)/shard_map/gather_step/pallas_call | solution.py:641
  127.7 0.0 copy-done.1
  127.7 0.0 copy-done.2
  127.7 2.9 %unpack.1 = (f32[3,32768]{1,0:T(4,128)}, f32[9,32768]{1,0:T(8,128)}) custom-call(s32[64]{0:T(128)S(1)} %copy-done.2, s32[64]{0:T(128)S(1)} %copy-done.1, bf16[128,48,128]{2,1,0:T(8,128)(2,1)S(1)} %gather_step.1.returned_ref), custom_call_target="tpu_custom_call" | custom-call | tf_op jit(solution)/shard_map/unpack/pallas_call | solution.py:683
Async XLA Ops:
  3.4 1.6 %copy-start.3 = (f32[9,32768]{1,0:T(8,128)S(1)}, f32[9,32768]{1,0:T(8,128)}, u32[]{:S(2)}) copy-start(f32[9,32768]{1,0:T(8,128)} %affine_ref.1) | copy-start | bytes 3538948
  5.0 1.0 copy-start.4
  6.0 1.0 copy-start.5
  7.1 1.0 copy-start.6
  8.1 0.9 copy-start.7
  9.0 0.7 copy-start.8
  9.7 0.7 copy-start.9
  10.4 0.7 copy-start.10
  11.0 70.4 %copy-start = (f32[32,4096]{1,0:T(8,128)S(1)}, f32[32,4096]{1,0:T(8,128)}, u32[]{:S(2)}) copy-start(f32[32,4096]{1,0:T(8,128)} %drag_ref.1) | copy-start | bytes 1572868
  86.2 41.5 %copy-start.1 = (s32[64]{0:T(128)S(1)}, s32[64]{0:T(128)}, u32[]{:S(2)}) copy-start(s32[64]{0:T(128)} %count_ref.3) | copy-start | bytes 772
  86.2 41.5 %copy-start.2 = (s32[64]{0:T(128)S(1)}, s32[64]{0:T(128)}, u32[]{:S(2)}) copy-start(s32[64]{0:T(128)} %get-tuple-element.20.dest_ref) | copy-start | bytes 772

commit v2 on v1

--- a/solution.py
+++ b/solution.py
@@ -13,6 +13,7 @@
 FIELDS = 16
 RESULTS = 12
 PARTS = 4
+UNROLL = 4
 GROUP_AXES = ("gy", "gz")
 F32 = jnp.float32
 BF16 = jnp.bfloat16
@@ -26,89 +27,6 @@
 
 def cost(flops):
     return pl.CostEstimate(flops=flops, bytes_accessed=1 << 22, transcendentals=0)
-
-
-def plan_kernel(
-    cap, owner_ref, slot_ref, count_ref, table_ref, live_ref, dest_ref, marks_ref, used_ref, tile_ref
-):
-    group = used_ref.shape[0]
-
-    def clear_used(i, carry):
-        used_ref[i] = 0
-        return carry
-
-    def clear_slots(i, carry):
-        table_ref[i] = 0
-        live_ref[i] = 0
-        tile_ref[i] = -1
-        return carry
-
-    lax.fori_loop(0, group, clear_used, 0)
-    lax.fori_loop(0, group * cap, clear_slots, 0, unroll=8)
-
-    def place(block, carry):
-        owner = owner_ref[block]
-        rank = used_ref[owner]
-        used_ref[owner] = rank + 1
-        where = owner * cap + rank
-        table_ref[where] = block
-        live_ref[where] = count_ref[block]
-        tile_ref[where] = slot_ref[block]
-        dest_ref[block] = where
-        return carry
-
-    lax.fori_loop(0, owner_ref.shape[0], place, 0)
-    lane = lax.broadcasted_iota(jnp.int32, (1, LANES), 1)
-
-    def mark(owner, carry):
-        row = jnp.full((1, LANES), -1, jnp.int32)
-        for i in range(cap):
-            row = jnp.where(lane == i, tile_ref[owner * cap + i], row)
-        marks_ref[owner] = row
-        return carry
-
-    lax.fori_loop(0, group, mark, 0)
-
-
-def plan(cap, group, owner, slot, count):
-    slots = group * cap
-    return pl.pallas_call(
-        functools.partial(plan_kernel, cap),
-        name="plan",
-        out_shape=(
-            jax.ShapeDtypeStruct((slots,), jnp.int32),
-            jax.ShapeDtypeStruct((slots,), jnp.int32),
-            jax.ShapeDtypeStruct(owner.shape, jnp.int32),
-            jax.ShapeDtypeStruct((group, 1, LANES), jnp.int32),
-        ),
-        in_specs=[SMEM] * 3,
-        out_specs=(SMEM, SMEM, SMEM, VMEM),
-        scratch_shapes=[pltpu.SMEM((group,), jnp.int32), pltpu.SMEM((slots,), jnp.int32)],
-    )(owner, slot, count)
-
-
-class Group:
-    def __init__(self):
-        self.wide = lax.axis_size(GROUP_AXES[1])
-        self.size = lax.axis_size(GROUP_AXES)
-        self.me = lax.axis_index(GROUP_AXES[0]) * self.wide + lax.axis_index(GROUP_AXES[1])
-
-    def device(self, peer):
-        return {GROUP_AXES[0]: peer // self.wide, GROUP_AXES[1]: peer % self.wide}
-
-    def greet(self):
-        barrier = pltpu.get_barrier_semaphore()
-
-        def signal(k, carry):
-            pl.semaphore_signal(
-                barrier, inc=1, device_id=self.device(self.me ^ k), device_id_type=MESH
-            )
-            return carry
-
-        lax.fori_loop(1, self.size, signal, 0)
-
-    def gathered(self):
-        pl.semaphore_wait(pltpu.get_barrier_semaphore(), self.size - 1)
 
 
 def twice(rows):
@@ -128,6 +46,155 @@
     )
     size = ((code & 127) + 128).astype(F32) * (scale * 2.0**-28)
     return jnp.where((code & 128) != 0, -size, size)
+
+
+def pack_kernel(
+    cap,
+    owner_ref,
+    slot_ref,
+    count_ref,
+    mass_ref,
+    velocity_ref,
+    affine_ref,
+    cell_ref,
+    fraction_ref,
+    packed_ref,
+    dest_ref,
+    marks_ref,
+    used_ref,
+    tile_ref,
+    stage_ref,
+    mass_v,
+    velocity_v,
+    affine_v,
+    cell_v,
+    fraction_v,
+    load_sems,
+):
+    sources = (mass_ref, velocity_ref, affine_ref, cell_ref, fraction_ref)
+    staged = (mass_v, velocity_v, affine_v, cell_v, fraction_v)
+    loads = [
+        pltpu.make_async_copy(source, target, load_sems.at[i])
+        for i, (source, target) in enumerate(zip(sources, staged))
+    ]
+    for load in loads:
+        load.start()
+    group = used_ref.shape[0]
+    blocks, _, width = mass_v.shape
+    quarters = width // LANES
+    rows = quarters * FIELDS
+
+    def clear_used(i, carry):
+        used_ref[i] = 0
+        return carry
+
+    def clear_slots(i, carry):
+        tile_ref[i] = -1
+        packed_ref[i] = jnp.zeros((rows, LANES), BF16)
+        return carry
+
+    lax.fori_loop(0, group, clear_used, 0, unroll=8)
+    lax.fori_loop(0, group * cap, clear_slots, 0, unroll=8)
+
+    def place(block, carry):
+        owner = owner_ref[block]
+        rank = used_ref[owner]
+        used_ref[owner] = rank + 1
+        where = owner * cap + rank
+        tile_ref[where] = slot_ref[block]
+        dest_ref[block] = where
+        return carry
+
+    lax.fori_loop(0, blocks, place, 0, unroll=2)
+    lane = lax.broadcasted_iota(jnp.int32, (1, LANES), 1)
+
+    def mark(owner, carry):
+        row = jnp.full((1, LANES), -1, jnp.int32)
+        for i in range(cap):
+            row = jnp.where(lane == i, tile_ref[owner * cap + i], row)
+        marks_ref[owner] = row
+        return carry
+
+    lax.fori_loop(0, group, mark, 0, unroll=2)
+    for load in loads:
+        load.wait()
+    place_lane = lax.broadcasted_iota(jnp.int32, (1, width), 1)
+
+    def pack(step, carry):
+        for u in range(UNROLL):
+            block = step * UNROLL + u
+            cols = pl.ds(pl.multiple_of(block * width, LANES), width)
+            live = jnp.where(place_lane < count_ref[block], mass_v[block], 0.0)
+            velocity = velocity_v[:, cols]
+            affine = affine_v[:, cols]
+            code = encode(cell_v[:, cols] * QUANT + fraction_v[:, cols])
+            for q in range(quarters):
+                base = u * rows + q * FIELDS
+                stage_ref[base : base + 1] = live[:, span_of(q)]
+                stage_ref[base + 1 : base + 4] = velocity[:, span_of(q)]
+                stage_ref[base + 4 : base + 13] = affine[:, span_of(q)]
+                stage_ref[base + 13 : base + 16] = code[:, span_of(q)]
+        for u in range(UNROLL):
+            packed_ref[dest_ref[step * UNROLL + u]] = stage_ref[
+                u * rows : (u + 1) * rows
+            ].astype(BF16)
+        return carry
+
+    lax.fori_loop(0, blocks // UNROLL, pack, 0)
+
+
+def pack(cap, group, owner, slot, count, mass, velocity, affine, cell, fraction):
+    slots = group * cap
+    blocks, _, width = mass.shape
+    rows = width // LANES * FIELDS
+    arrays = (mass, velocity, affine, cell, fraction)
+    return pl.pallas_call(
+        functools.partial(pack_kernel, cap),
+        name="pack",
+        out_shape=(
+            pltpu.VMEM((slots, rows, LANES), BF16),
+            jax.ShapeDtypeStruct(owner.shape, jnp.int32),
+            pltpu.VMEM((group, 1, LANES), jnp.int32),
+        ),
+        in_specs=[SMEM] * 3 + [HBM] * 5,
+        out_specs=(VMEM, SMEM, VMEM),
+        scratch_shapes=[
+            pltpu.SMEM((group,), jnp.int32),
+            pltpu.SMEM((slots,), jnp.int32),
+            pltpu.VMEM((UNROLL * rows, LANES), F32),
+        ]
+        + [pltpu.VMEM(array.shape, array.dtype) for array in arrays]
+        + [pltpu.SemaphoreType.DMA((len(arrays),))],
+        compiler_params=pltpu.CompilerParams(vmem_limit_bytes=60 << 20),
+    )(owner, slot, count, *arrays)
+
+
+def pieces(subs):
+    return [(0, 1), (1, 1), (2, 2)] if subs == 4 else [(sub, 1) for sub in range(subs)]
+
+
+class Group:
+    def __init__(self):
+        self.wide = lax.axis_size(GROUP_AXES[1])
+        self.size = lax.axis_size(GROUP_AXES)
+        self.me = lax.axis_index(GROUP_AXES[0]) * self.wide + lax.axis_index(GROUP_AXES[1])
+
+    def device(self, peer):
+        return {GROUP_AXES[0]: peer // self.wide, GROUP_AXES[1]: peer % self.wide}
+
+    def greet(self):
+        barrier = pltpu.get_barrier_semaphore()
+
+        def signal(k, carry):
+            pl.semaphore_signal(
+                barrier, inc=1, device_id=self.device(self.me ^ k), device_id_type=MESH
+            )
+            return carry
+
+        lax.fori_loop(1, self.size, signal, 0)
+
+    def gathered(self):
+        pl.semaphore_wait(pltpu.get_barrier_semaphore(), self.size - 1)
 
 
 def decode(value):
@@ -274,27 +341,13 @@
 def scatter_kernel(
     cap,
     subs,
-    table_ref,
-    live_ref,
+    packed_ref,
     marks_ref,
-    mass_ref,
-    velocity_ref,
-    affine_ref,
-    cell_ref,
-    fraction_ref,
     arrived_ref,
     sums_ref,
     told_ref,
-    mass_v,
-    velocity_v,
-    affine_v,
-    cell_v,
-    fraction_v,
-    stage_ref,
-    packed_ref,
     fields_ref,
     rows_ref,
-    load_sems,
     send_sems,
     recv_sems,
     mark_send,
@@ -303,41 +356,7 @@
     group = Group()
     n, me = group.size, group.me
     per = cap // subs
-    blocks, _, width = mass_v.shape
-    quarters = width // LANES
-    sources = (velocity_ref, affine_ref, cell_ref, fraction_ref)
-    staged = (velocity_v, affine_v, cell_v, fraction_v)
-    mass_load = pltpu.make_async_copy(mass_ref, mass_v, load_sems.at[len(sources)])
-    mass_load.start()
-
-    def load_block(block, carry):
-        cols = pl.ds(pl.multiple_of(block * width, LANES), width)
-        for i, (source, target) in enumerate(zip(sources, staged)):
-            pltpu.make_async_copy(
-                source.at[:, cols], target.at[block], load_sems.at[i]
-            ).start()
-        return carry
-
-    lax.fori_loop(0, blocks, load_block, 0, unroll=4)
     group.greet()
-    lane = lax.broadcasted_iota(jnp.int32, (1, width), 1)
-    mass_load.wait()
-    for i, target in enumerate(staged):
-        pltpu.make_async_copy(target, target, load_sems.at[i]).wait()
-
-    def pack(slot):
-        block = table_ref[slot]
-        live = jnp.where(lane < live_ref[slot], mass_v[block], 0.0)
-        velocity = velocity_v[block]
-        affine = affine_v[block]
-        code = encode(cell_v[block] * QUANT + fraction_v[block])
-        for q in range(quarters):
-            base = q * FIELDS
-            stage_ref[base : base + 1] = live[:, span_of(q)]
-            stage_ref[base + 1 : base + 4] = velocity[:, span_of(q)]
-            stage_ref[base + 4 : base + 13] = affine[:, span_of(q)]
-            stage_ref[base + 13 : base + 16] = code[:, span_of(q)]
-        packed_ref[slot] = stage_ref[...].astype(BF16)
 
     def rows_of(device, sub):
         return pl.ds(device * cap + sub * per, per)
@@ -373,46 +392,34 @@
     own_marks = pltpu.make_async_copy(marks_ref.at[me], told_ref.at[me], mark_recv.at[0])
     own_marks.start()
 
-    def pack_step(step):
-        k = n - 1 - step % n
-        sub = step // n
-        for i in range(per):
-            pack((me ^ k) * cap + sub * per + i)
-
-    def send_step(step):
-        k = n - 1 - step % n
-        sub = step // n
-
-        @pl.when(k != 0)
-        def _():
-            transfer(k, sub).start()
-
-        @pl.when(k == 0)
-        def _():
-            arrival(0, sub).start()
-
-    pack_step(0)
+    for sub in range(subs):
+        arrival(0, sub).start()
     group.gathered()
-
-    def pack_and_send(step, carry):
-        pack_step(step)
-        send_step(step - 1)
-        return carry
-
-    lax.fori_loop(1, n * subs, pack_and_send, 0)
+    half = n // 2
+
+    def send_near(step, carry):
+        transfer(1 + step // subs, step % subs).start()
+        return carry
+
+    def send_far(step, carry):
+        transfer(half + step % half, step // half).start()
+        return carry
 
     def send_marks(k, carry):
         mark_transfer(k).start()
         return carry
 
+    lax.fori_loop(0, (half - 1) * subs, send_near, 0)
+    lax.fori_loop(0, half * subs, send_far, 0)
     lax.fori_loop(1, n, send_marks, 0)
-    send_step(n * subs - 1)
-
     pair = 2
+    strides = half // pair
 
     def take(step, carry):
-        sub = step // (n // pair)
-        first = (step % (n // pair)) * pair
+        side = step // (strides * subs)
+        rest = step % (strides * subs)
+        sub = (1 - side) * (rest % subs) + side * (rest // strides)
+        first = side * half + pair * ((1 - side) * (rest // subs) + side * (rest % strides))
         for j in range(pair):
             arrival(first + j, sub).wait()
         for j in range(pair):
@@ -423,7 +430,7 @@
                 )
         return carry
 
-    lax.fori_loop(0, n // pair * subs, take, 0)
+    lax.fori_loop(0, strides * subs * 2, take, 0)
     own_marks.wait()
 
     def settle(k, carry):
@@ -436,47 +443,39 @@
     lax.fori_loop(1, n, settle, 0)
 
 
-def scatter(cap, subs, group, table, live, marks, mass, velocity, affine, cell, fraction):
-    slots = group * cap
-    blocks, _, width = mass.shape
-    quarters = width // LANES
-    rows = quarters * FIELDS
+def scatter(cap, subs, packed, marks):
+    slots, rows, _ = packed.shape
+    group = marks.shape[0]
+    quarters = rows // FIELDS
     unroll = 2 * (cap // subs)
-    arrays = (mass, velocity, affine, cell, fraction)
     return pl.pallas_call(
         functools.partial(scatter_kernel, cap, subs),
         name="scatter_step",
         out_shape=(
-            jax.ShapeDtypeStruct((slots, rows, LANES), BF16),
+            jax.ShapeDtypeStruct(packed.shape, BF16),
             jax.ShapeDtypeStruct((slots, 4 * EDGE, EDGE * EDGE), F32),
             jax.ShapeDtypeStruct(marks.shape, jnp.int32),
         ),
-        in_specs=[SMEM, SMEM, VMEM] + [HBM] * 5,
+        in_specs=[VMEM, VMEM],
         out_specs=(VMEM,) * 3,
-        scratch_shapes=[pltpu.VMEM(mass.shape, F32)]
-        + [
-            pltpu.VMEM((blocks, array.shape[0], width), array.dtype) for array in arrays[1:]
-        ]
-        + [
-            pltpu.VMEM((rows, LANES), F32),
-            pltpu.VMEM((slots, rows, LANES), BF16),
+        scratch_shapes=[
             pltpu.VMEM((unroll * rows, LANES), F32),
             pltpu.VMEM((unroll * 2 * quarters * EDGE, LANES), F32),
-            pltpu.SemaphoreType.DMA((len(arrays),)),
             pltpu.SemaphoreType.DMA((group, subs)),
             pltpu.SemaphoreType.DMA((group, subs)),
             pltpu.SemaphoreType.DMA((group,)),
             pltpu.SemaphoreType.DMA((group,)),
         ],
         compiler_params=pltpu.CompilerParams(
-            collective_id=0, has_side_effects=True, vmem_limit_bytes=40 << 20
+            collective_id=0, has_side_effects=True, vmem_limit_bytes=30 << 20
         ),
         cost_estimate=cost(10**10),
-    )(table, live, marks, *arrays)
-
-
-def grid_kernel(cap, told_ref, deposits_ref, drag_ref, grid_ref, round_ref, sums_ref):
+    )(packed, marks)
+
+
+def grid_kernel(cap, told_ref, deposits_ref, drag_ref, ratio_ref, round_ref, sums_ref):
     plane_size = EDGE * EDGE
+    tiles = drag_ref.shape[0]
 
     def start(t, carry):
         for x in range(EDGE):
@@ -486,32 +485,28 @@
         sums_ref[t, EDGE:, :] = jnp.zeros((3 * EDGE, plane_size), F32)
         return carry
 
-    lax.fori_loop(0, drag_ref.shape[0], start, 0)
+    lax.fori_loop(0, tiles, start, 0, unroll=2)
+    sums_ref[tiles] = jnp.zeros((4 * EDGE, plane_size), F32)
 
     def add(device, carry):
         for i in range(cap):
-            tile = told_ref[device, 0, i]
-
-            @pl.when(tile >= 0)
-            def _():
-                sums_ref[tile] += deposits_ref[device * cap + i]
-
+            mark = told_ref[device, 0, i]
+            tile = jnp.where(mark < 0, tiles, mark)
+            sums_ref[tile] += deposits_ref[device * cap + i]
         return carry
 
     lax.fori_loop(0, told_ref.shape[0], add, 0)
 
     def divide(t, carry):
         mass = sums_ref[t, :EDGE, :]
-        parts = [sums_ref[t, (d + 1) * EDGE : (d + 2) * EDGE, :] / mass for d in range(3)]
-        round_ref[t] = jnp.concatenate(parts, axis=0).astype(BF16)
-        for d in range(3):
-            for x in range(EDGE):
-                grid_ref[d, pl.ds(t, 1), x * plane_size : (x + 1) * plane_size] = parts[d][
-                    x : x + 1
-                ]
-        return carry
-
-    lax.fori_loop(0, round_ref.shape[0], divide, 0)
+        ratio = jnp.concatenate(
+            [sums_ref[t, (d + 1) * EDGE : (d + 2) * EDGE, :] / mass for d in range(3)], axis=0
+        )
+        ratio_ref[t] = ratio
+        round_ref[t] = ratio.astype(BF16)
+        return carry
+
+    lax.fori_loop(0, tiles, divide, 0, unroll=2)
 
 
 def grid_step(cap, told, deposits, drag):
@@ -521,12 +516,12 @@
         functools.partial(grid_kernel, cap),
         name="grid_step",
         out_shape=(
-            jax.ShapeDtypeStruct((3, tiles, EDGE * plane_size), F32),
-            jax.ShapeDtypeStruct((tiles, 3 * EDGE, plane_size), BF16),
+            pltpu.VMEM((tiles, 3 * EDGE, plane_size), F32),
+            pltpu.VMEM((tiles, 3 * EDGE, plane_size), BF16),
         ),
         in_specs=[SMEM, VMEM, VMEM],
         out_specs=(VMEM, VMEM),
-        scratch_shapes=[pltpu.VMEM((tiles, 4 * EDGE, plane_size), F32)],
+        scratch_shapes=[pltpu.VMEM((tiles + 1, 4 * EDGE, plane_size), F32)],
         compiler_params=pltpu.CompilerParams(vmem_limit_bytes=20 << 20),
         cost_estimate=cost(10**9),
     )(told, deposits, drag)
@@ -538,7 +533,9 @@
     told_ref,
     arrived_ref,
     round_ref,
+    ratio_ref,
     returned_ref,
+    grid_ref,
     results_ref,
     fields_ref,
     rows_ref,
@@ -550,25 +547,27 @@
     n, me = group.size, group.me
     per = cap // subs
     group.greet()
-
-    def rows_of(device, sub):
-        return pl.ds(device * cap + sub * per, per)
-
-    def transfer(k, sub):
+    cuts = pieces(subs)
+
+    def rows_of(device, piece):
+        first, length = cuts[piece]
+        return pl.ds(device * cap + first * per, length * per)
+
+    def transfer(k, piece):
         peer = me ^ k
         return pltpu.make_async_remote_copy(
-            src_ref=results_ref.at[rows_of(peer, sub)],
-            dst_ref=returned_ref.at[rows_of(me, sub)],
-            send_sem=send_sems.at[k, sub],
-            recv_sem=recv_sems.at[k, sub],
+            src_ref=results_ref.at[rows_of(peer, piece)],
+            dst_ref=returned_ref.at[rows_of(me, piece)],
+            send_sem=send_sems.at[k, piece],
+            recv_sem=recv_sems.at[k, piece],
             device_id=group.device(peer),
             device_id_type=MESH,
         )
 
-    def arrival(k, sub):
-        rows = rows_of(me ^ k, sub)
+    def arrival(k, piece):
+        rows = rows_of(me ^ k, piece)
         return pltpu.make_async_copy(
-            results_ref.at[rows], returned_ref.at[rows], recv_sems.at[k, sub]
+            results_ref.at[rows], returned_ref.at[rows], recv_sems.at[k, piece]
         )
 
     pair = 2
@@ -598,16 +597,17 @@
 
     def send(step):
         top, sub = place(step)
-        for j in range(pair):
-            k = top - j
-
-            @pl.when(k != 0)
-            def _():
-                transfer(k, sub).start()
-
-            @pl.when(k == 0)
-            def _():
-                arrival(0, sub).start()
+        for piece, (first, length) in enumerate(cuts):
+            for j in range(pair):
+                k = top - j
+
+                @pl.when((sub == first + length - 1) & (k != 0))
+                def _():
+                    transfer(k, piece).start()
+
+                @pl.when((sub == first + length - 1) & (k == 0))
+                def _():
+                    arrival(0, piece).start()
 
     steps = half // pair * subs * 2
     work(0)
@@ -621,18 +621,31 @@
     lax.fori_loop(1, steps, work_and_send, 0)
     send(steps - 1)
 
+    plane_size = EDGE * EDGE
+
+    def spread_rows(t, carry):
+        for d in range(3):
+            for x in range(EDGE):
+                row = d * EDGE + x
+                grid_ref[d, pl.ds(t, 1), x * plane_size : (x + 1) * plane_size] = ratio_ref[
+                    t, row : row + 1, :
+                ]
+        return carry
+
+    lax.fori_loop(0, ratio_ref.shape[0], spread_rows, 0)
+
     def settle(k, carry):
-        for sub in range(subs):
-            transfer(k, sub).wait_recv()
-            transfer(k, sub).wait_send()
-        return carry
-
-    for sub in range(subs):
-        arrival(0, sub).wait()
+        for piece in range(len(cuts)):
+            transfer(k, piece).wait_recv()
+            transfer(k, piece).wait_send()
+        return carry
+
+    for piece in range(len(cuts)):
+        arrival(0, piece).wait()
     lax.fori_loop(1, n, settle, 0)
 
 
-def gather(cap, subs, told, arrived, rounded):
+def gather(cap, subs, told, arrived, rounded, ratio):
     slots, rows, _ = arrived.shape
     group = told.shape[0]
     quarters = rows // FIELDS
@@ -641,9 +654,12 @@
     return pl.pallas_call(
         functools.partial(gather_kernel, cap, subs),
         name="gather_step",
-        out_shape=jax.ShapeDtypeStruct(result, BF16),
-        in_specs=[SMEM, VMEM, VMEM],
-        out_specs=VMEM,
+        out_shape=(
+            pltpu.VMEM(result, BF16),
+            pltpu.VMEM((3, ratio.shape[0], EDGE**3), F32),
+        ),
+        in_specs=[SMEM, VMEM, VMEM, VMEM],
+        out_specs=(VMEM, VMEM),
         scratch_shapes=[
             pltpu.VMEM(result, BF16),
             pltpu.VMEM((unroll * rows, LANES), F32),
@@ -656,10 +672,23 @@
             collective_id=1, has_side_effects=True, vmem_limit_bytes=40 << 20
         ),
         cost_estimate=cost(10**10),
-    )(told, arrived, rounded)
-
-
-def unpack_kernel(dest_ref, count_ref, returned_ref, velocity_ref, affine_ref):
+    )(told, arrived, rounded, ratio)
+
+
+def unpack_kernel(
+    dest_ref,
+    count_ref,
+    returned_ref,
+    grid_ref,
+    velocity_out,
+    affine_out,
+    grid_out,
+    velocity_ref,
+    affine_ref,
+    sems,
+):
+    copies = [pltpu.make_async_copy(grid_ref, grid_out, sems.at[0, 0])]
+    copies[0].start()
     blocks = dest_ref.shape[0]
     width = velocity_ref.shape[1] // blocks
     lane = lax.broadcasted_iota(jnp.int32, (1, LANES), 1)
@@ -675,22 +704,39 @@
             affine_ref[:, cols] = part[3:]
         return carry
 
-    lax.fori_loop(0, blocks, unpack, 0)
-
-
-def unpack(dest, count, returned, width):
+    share = blocks // PARTS
+    for c in range(PARTS):
+        lax.fori_loop(c * share, (c + 1) * share, unpack, 0, unroll=4)
+        cols = pl.ds(c * share * width, share * width)
+        for i, (source, target) in enumerate(
+            ((velocity_ref, velocity_out), (affine_ref, affine_out))
+        ):
+            copy = pltpu.make_async_copy(
+                source.at[:, cols], target.at[:, cols], sems.at[i + 1, c]
+            )
+            copy.start()
+            copies.append(copy)
+    for copy in copies:
+        copy.wait()
+
+
+def unpack(dest, count, returned, grid, width):
     particles = dest.shape[0] * width
+    velocity = jax.ShapeDtypeStruct((3, particles), F32)
+    affine = jax.ShapeDtypeStruct((9, particles), F32)
     return pl.pallas_call(
         unpack_kernel,
         name="unpack",
-        out_shape=(
-            jax.ShapeDtypeStruct((3, particles), F32),
-            jax.ShapeDtypeStruct((9, particles), F32),
-        ),
-        in_specs=[SMEM, SMEM, VMEM],
-        out_specs=(VMEM, VMEM),
+        out_shape=(velocity, affine, jax.ShapeDtypeStruct(grid.shape, F32)),
+        in_specs=[SMEM, SMEM, VMEM, VMEM],
+        out_specs=(HBM, HBM, HBM),
+        scratch_shapes=[
+            pltpu.VMEM(velocity.shape, F32),
+            pltpu.VMEM(affine.shape, F32),
+            pltpu.SemaphoreType.DMA((3, PARTS)),
+        ],
         compiler_params=pltpu.CompilerParams(vmem_limit_bytes=20 << 20),
-    )(dest, count, returned)
+    )(dest, count, returned, grid)
 
 
 def per_device(
@@ -709,23 +755,22 @@
     width = particle_mass.shape[0] // blocks
     cap = max(1, 2 * blocks // group)
     subs = min(cap, PARTS)
-    table, live, dest, marks = plan(cap, group, block_owner[:, 0], block_slot, block_count)
-    arrived, deposits, told = scatter(
+    packed, dest, marks = pack(
         cap,
-        subs,
         group,
-        table,
-        live,
-        marks,
+        block_owner[:, 0],
+        block_slot,
+        block_count,
         particle_mass.reshape(blocks, 1, width),
         particle_velocity,
         particle_affine,
         particle_cell,
         particle_fraction,
     )
-    grid_velocity, rounded = grid_step(cap, told, deposits, cell_drag)
-    returned = gather(cap, subs, told, arrived, rounded)
-    new_velocity, new_affine = unpack(dest, block_count, returned, width)
+    arrived, deposits, told = scatter(cap, subs, packed, marks)
+    ratio, rounded = grid_step(cap, told, deposits, cell_drag)
+    returned, grid = gather(cap, subs, told, arrived, rounded, ratio)
+    new_velocity, new_affine, grid_velocity = unpack(dest, block_count, returned, grid, width)
     return jnp.transpose(grid_velocity, (1, 0, 2)), new_velocity, new_affine
 
 

time: 131 us -> 108 us (0.82)
  Pallas kernels: 122 us -> 107 us
  local copies, waits for them, and re-layouts: 7.63 us -> 0.02 us
    pallas_call x1, Pallas kernels: 70.4 us -> 55.2 us  [scatter(): pl.pallas_call(functools.partial(scatter_kernel, cap, subs), name='scatte...]
    unnamed x22 -> x6, local copies, waits for them, and re-layouts: 7.63 us -> 0.02 us
    pallas_call x1, Pallas kernels: 4.78 us -> 2.44 us  [grid_step(): pl.pallas_call(functools.partial(grid_kernel, cap), name='grid_step', out...]
where the time goes in v2:
time: 108 us
  Pallas kernels  107 us (99%)
    pallas_call x1, Pallas kernels, scatter(): pl.pallas_call(functools.partial(scatter_kernel, cap, subs), name='scatte...  55.2 us
    pallas_call x1, Pallas kernels, gather(): pl.pallas_call(functools.partial(gather_kernel, cap, subs), name='gather_...  42.4 us
    pallas_call x1, Pallas kernels, pack(): pl.pallas_call(functools.partial(pack_kernel, cap), name='pack', out_shap...  4.25 us
    pallas_call x1, Pallas kernels, unpack(): pl.pallas_call(unpack_kernel, name='unpack', out_shape=(velocity, affine,...  2.65 us
    pallas_call x1, Pallas kernels, grid_step(): pl.pallas_call(functools.partial(grid_kernel, cap), name='grid_step', out...  2.44 us

profile of v2, /device:TPU:0, one launch (start us, length us, event | category | flops | bytes accessed | tf_op | source)
XLA Modules:
  0.0 107.7 jit_solution(388718350212874016)
XLA Ops:
  0.6 4.2 %pack.1 = (bf16[128,64,128]{2,1,0:T(8,128)(2,1)S(1)}, s32[64]{0:T(128)}, s32[16,1,128]{2,1,0:T(1,128)S(1)}) custom-call(s32[64]{0:T(128)} %bitcast.4, s32[64]{0:T(128)} %slot_ref.1, s32[64]{0:T(128)} %count_ref.3, f32[64,1,512]{2,1,0:T(1,128)} %bitcast.3, f32[3,32768]{1,0:T(4,128)} %velocity_ref.1, f32[9,32768]{1,0:T(8,128)} %affine_ref.1, ...), custom_call_target="tpu_custom_call" | custom-call | tf_op jit(solution)/shard_map/pack/pallas_call | solution.py:151
  4.9 0.0 copy-start
  4.9 55.2 %scatter_step.1 = (bf16[128,64,128]{2,1,0:T(8,128)(2,1)S(1)}, f32[128,64,256]{2,1,0:T(8,128)S(1)}, s32[16,1,128]{2,1,0:T(1,128)S(1)}) custom-call(bf16[128,64,128]{2,1,0:T(8,128)(2,1)S(1)} %get-tuple-element.17.packed_ref, s32[16,1,128]{2,1,0:T(1,128)S(1)} %get-tuple-element.18.marks_ref), custom_call_target="tpu_custom_call" | custom-call | flops 10000000000 | bytes 4194304 | tf_op jit(solution)/shard_map/scatter_step/pallas_call | solution.py:451
  60.1 0.0 copy-done
  60.1 2.4 %grid_step.1 = (f32[32,48,256]{2,1,0:T(8,128)S(1)}, bf16[32,48,256]{2,1,0:T(8,128)(2,1)S(1)}) custom-call(s32[16,1,128]{2,1,0:T(1,128)S(1)} %get-tuple-element.19.told_ref, f32[128,64,256]{2,1,0:T(8,128)S(1)} %get-tuple-element.21.deposits_ref, f32[32,4096]{1,0:T(8,128)S(1)} %copy-done), custom_call_target="tpu_custom_call" | custom-call | flops 1000000000 | bytes 4194304 | tf_op jit(solution)/shard_map/grid_step/pallas_call | solution.py:515
  62.5 0.0 copy-start.1
  62.5 0.0 copy-start.2
  62.6 42.4 %gather_step.1 = (bf16[128,48,128]{2,1,0:T(8,128)(2,1)S(1)}, f32[3,32,4096]{2,1,0:T(8,128)S(1)}) custom-call(s32[16,1,128]{2,1,0:T(1,128)S(1)} %get-tuple-element.19.told_ref, bf16[128,64,128]{2,1,0:T(8,128)(2,1)S(1)} %get-tuple-element.20.arrived_ref, bf16[32,48,256]{2,1,0:T(8,128)(2,1)S(1)} %get-tuple-element.22.round_ref, ...), custom_call_target="tpu_custom_call" | custom-call | flops 10000000000 | bytes 4194304 | tf_op jit(solution)/shard_map/gather_step/pallas_call | solution.py:654
  105.0 0.0 copy-done.1
  105.0 0.0 copy-done.2
  105.0 2.6 %unpack.1 = (f32[3,32768]{1,0:T(4,128)}, f32[9,32768]{1,0:T(8,128)}, f32[3,32,4096]{2,1,0:T(8,128)}) custom-call(s32[64]{0:T(128)S(1)} %copy-done.2, s32[64]{0:T(128)S(1)} %copy-done.1, bf16[128,48,128]{2,1,0:T(8,128)(2,1)S(1)} %get-tuple-element.24.returned_ref, f32[3,32,4096]{2,1,0:T(8,128)S(1)} %get-tuple-element.25.grid_ref), custom_call_target="tpu_custom_call" | custom-call | tf_op jit(solution)/shard_map/unpack/pallas_call | solution.py:727
Async XLA Ops:
  4.9 55.2 %copy-start = (f32[32,4096]{1,0:T(8,128)S(1)}, f32[32,4096]{1,0:T(8,128)}, u32[]{:S(2)}) copy-start(f32[32,4096]{1,0:T(8,128)} %drag_ref.1) | copy-start | bytes 1572868
  62.5 42.5 %copy-start.1 = (s32[64]{0:T(128)S(1)}, s32[64]{0:T(128)}, u32[]{:S(2)}) copy-start(s32[64]{0:T(128)} %count_ref.3) | copy-start | bytes 772
  62.5 42.5 %copy-start.2 = (s32[64]{0:T(128)S(1)}, s32[64]{0:T(128)}, u32[]{:S(2)}) copy-start(s32[64]{0:T(128)} %get-tuple-element.16.dest_ref) | copy-start | bytes 772

commit v3 on v2

--- a/solution.py
+++ b/solution.py
@@ -73,14 +73,20 @@
 ):
     sources = (mass_ref, velocity_ref, affine_ref, cell_ref, fraction_ref)
     staged = (mass_v, velocity_v, affine_v, cell_v, fraction_v)
-    loads = [
-        pltpu.make_async_copy(source, target, load_sems.at[i])
-        for i, (source, target) in enumerate(zip(sources, staged))
-    ]
+    blocks, _, width = mass_v.shape
+    share = blocks // PARTS
+    loads = []
+    for c in range(PARTS):
+        rows = pl.ds(c * share, share)
+        cols = pl.ds(c * share * width, share * width)
+        for i, (source, target) in enumerate(zip(sources, staged)):
+            part = rows if i == 0 else (slice(None), cols)
+            loads.append(
+                pltpu.make_async_copy(source.at[part], target.at[part], load_sems.at[i, c])
+            )
     for load in loads:
         load.start()
     group = used_ref.shape[0]
-    blocks, _, width = mass_v.shape
     quarters = width // LANES
     rows = quarters * FIELDS
 
@@ -116,8 +122,6 @@
         return carry
 
     lax.fori_loop(0, group, mark, 0, unroll=2)
-    for load in loads:
-        load.wait()
     place_lane = lax.broadcasted_iota(jnp.int32, (1, width), 1)
 
     def pack(step, carry):
@@ -140,7 +144,10 @@
             ].astype(BF16)
         return carry
 
-    lax.fori_loop(0, blocks // UNROLL, pack, 0)
+    for c in range(PARTS):
+        for load in loads[c * len(sources) : (c + 1) * len(sources)]:
+            load.wait()
+        lax.fori_loop(c * share // UNROLL, (c + 1) * share // UNROLL, pack, 0)
 
 
 def pack(cap, group, owner, slot, count, mass, velocity, affine, cell, fraction):
@@ -164,13 +171,9 @@
             pltpu.VMEM((UNROLL * rows, LANES), F32),
         ]
         + [pltpu.VMEM(array.shape, array.dtype) for array in arrays]
-        + [pltpu.SemaphoreType.DMA((len(arrays),))],
+        + [pltpu.SemaphoreType.DMA((len(arrays), PARTS))],
         compiler_params=pltpu.CompilerParams(vmem_limit_bytes=60 << 20),
     )(owner, slot, count, *arrays)
-
-
-def pieces(subs):
-    return [(0, 1), (1, 1), (2, 2)] if subs == 4 else [(sub, 1) for sub in range(subs)]
 
 
 class Group:
@@ -547,27 +550,25 @@
     n, me = group.size, group.me
     per = cap // subs
     group.greet()
-    cuts = pieces(subs)
-
-    def rows_of(device, piece):
-        first, length = cuts[piece]
-        return pl.ds(device * cap + first * per, length * per)
-
-    def transfer(k, piece):
+
+    def rows_of(device, sub):
+        return pl.ds(device * cap + sub * per, per)
+
+    def transfer(k, sub):
         peer = me ^ k
         return pltpu.make_async_remote_copy(
-            src_ref=results_ref.at[rows_of(peer, piece)],
-            dst_ref=returned_ref.at[rows_of(me, piece)],
-            send_sem=send_sems.at[k, piece],
-            recv_sem=recv_sems.at[k, piece],
+            src_ref=results_ref.at[rows_of(peer, sub)],
+            dst_ref=returned_ref.at[rows_of(me, sub)],
+            send_sem=send_sems.at[k, sub],
+            recv_sem=recv_sems.at[k, sub],
             device_id=group.device(peer),
             device_id_type=MESH,
         )
 
-    def arrival(k, piece):
-        rows = rows_of(me ^ k, piece)
+    def arrival(k, sub):
+        rows = rows_of(me ^ k, sub)
         return pltpu.make_async_copy(
-            results_ref.at[rows], returned_ref.at[rows], recv_sems.at[k, piece]
+            results_ref.at[rows], returned_ref.at[rows], recv_sems.at[k, sub]
         )
 
     pair = 2
@@ -597,25 +598,29 @@
 
     def send(step):
         top, sub = place(step)
-        for piece, (first, length) in enumerate(cuts):
-            for j in range(pair):
-                k = top - j
-
-                @pl.when((sub == first + length - 1) & (k != 0))
-                def _():
-                    transfer(k, piece).start()
-
-                @pl.when((sub == first + length - 1) & (k == 0))
-                def _():
-                    arrival(0, piece).start()
+        for j in range(pair):
+            k = top - j
+
+            @pl.when(k != 0)
+            def _():
+                transfer(k, sub).start()
+
+            @pl.when(k == 0)
+            def _():
+                arrival(0, sub).start()
 
     steps = half // pair * subs * 2
     work(0)
     group.gathered()
+    send(0)
 
     def work_and_send(step, carry):
         work(step)
-        send(step - 1)
+
+        @pl.when(step > 1)
+        def _():
+            send(step - 1)
+
         return carry
 
     lax.fori_loop(1, steps, work_and_send, 0)
@@ -635,13 +640,13 @@
     lax.fori_loop(0, ratio_ref.shape[0], spread_rows, 0)
 
     def settle(k, carry):
-        for piece in range(len(cuts)):
-            transfer(k, piece).wait_recv()
-            transfer(k, piece).wait_send()
-        return carry
-
-    for piece in range(len(cuts)):
-        arrival(0, piece).wait()
+        for sub in range(subs):
+            transfer(k, sub).wait_recv()
+            transfer(k, sub).wait_send()
+        return carry
+
+    for sub in range(subs):
+        arrival(0, sub).wait()
     lax.fori_loop(1, n, settle, 0)
 
 

time: 108 us -> 106 us (0.981)
  Pallas kernels: 107 us -> 105 us
    pallas_call x1, Pallas kernels: 42.4 us -> 41.1 us  [gather(): pl.pallas_call(functools.partial(gather_kernel, cap, subs), name='gather_...]
where the time goes in v3:
time: 106 us
  Pallas kernels  105 us (99%)
    pallas_call x1, Pallas kernels, scatter(): pl.pallas_call(functools.partial(scatter_kernel, cap, subs), name='scatte...  55.2 us
    pallas_call x1, Pallas kernels, gather(): pl.pallas_call(functools.partial(gather_kernel, cap, subs), name='gather_...  41.1 us
    pallas_call x1, Pallas kernels, pack(): pl.pallas_call(functools.partial(pack_kernel, cap), name='pack', out_shap...  3.65 us
    pallas_call x1, Pallas kernels, unpack(): pl.pallas_call(unpack_kernel, name='unpack', out_shape=(velocity, affine,...  2.65 us
    pallas_call x1, Pallas kernels, grid_step(): pl.pallas_call(functools.partial(grid_kernel, cap), name='grid_step', out...  2.43 us

profile of v3, /device:TPU:0, one launch (start us, length us, event | category | flops | bytes accessed | tf_op | source)
XLA Modules:
  0.0 105.7 jit_solution(5227165698710464672)
XLA Ops:
  0.6 3.7 %pack.1 = (bf16[128,64,128]{2,1,0:T(8,128)(2,1)S(1)}, s32[64]{0:T(128)}, s32[16,1,128]{2,1,0:T(1,128)S(1)}) custom-call(s32[64]{0:T(128)} %bitcast.4, s32[64]{0:T(128)} %slot_ref.1, s32[64]{0:T(128)} %count_ref.3, f32[64,1,512]{2,1,0:T(1,128)} %bitcast.3, f32[3,32768]{1,0:T(4,128)} %velocity_ref.1, f32[9,32768]{1,0:T(8,128)} %affine_ref.1, ...), custom_call_target="tpu_custom_call" | custom-call | tf_op jit(solution)/shard_map/pack/pallas_call | solution.py:158
  4.3 0.0 copy-start
  4.3 55.2 %scatter_step.1 = (bf16[128,64,128]{2,1,0:T(8,128)(2,1)S(1)}, f32[128,64,256]{2,1,0:T(8,128)S(1)}, s32[16,1,128]{2,1,0:T(1,128)S(1)}) custom-call(bf16[128,64,128]{2,1,0:T(8,128)(2,1)S(1)} %get-tuple-element.17.packed_ref, s32[16,1,128]{2,1,0:T(1,128)S(1)} %get-tuple-element.18.marks_ref), custom_call_target="tpu_custom_call" | custom-call | flops 10000000000 | bytes 4194304 | tf_op jit(solution)/shard_map/scatter_step/pallas_call | solution.py:454
  59.5 0.0 copy-done
  59.5 2.4 %grid_step.1 = (f32[32,48,256]{2,1,0:T(8,128)S(1)}, bf16[32,48,256]{2,1,0:T(8,128)(2,1)S(1)}) custom-call(s32[16,1,128]{2,1,0:T(1,128)S(1)} %get-tuple-element.19.told_ref, f32[128,64,256]{2,1,0:T(8,128)S(1)} %get-tuple-element.21.deposits_ref, f32[32,4096]{1,0:T(8,128)S(1)} %copy-done), custom_call_target="tpu_custom_call" | custom-call | flops 1000000000 | bytes 4194304 | tf_op jit(solution)/shard_map/grid_step/pallas_call | solution.py:518
  61.9 0.0 copy-start.1
  61.9 0.0 copy-start.2
  61.9 41.1 %gather_step.1 = (bf16[128,48,128]{2,1,0:T(8,128)(2,1)S(1)}, f32[3,32,4096]{2,1,0:T(8,128)S(1)}) custom-call(s32[16,1,128]{2,1,0:T(1,128)S(1)} %get-tuple-element.19.told_ref, bf16[128,64,128]{2,1,0:T(8,128)(2,1)S(1)} %get-tuple-element.20.arrived_ref, bf16[32,48,256]{2,1,0:T(8,128)(2,1)S(1)} %get-tuple-element.22.round_ref, ...), custom_call_target="tpu_custom_call" | custom-call | flops 10000000000 | bytes 4194304 | tf_op jit(solution)/shard_map/gather_step/pallas_call | solution.py:659
  103.1 0.0 copy-done.1
  103.1 0.0 copy-done.2
  103.1 2.6 %unpack.1 = (f32[3,32768]{1,0:T(4,128)}, f32[9,32768]{1,0:T(8,128)}, f32[3,32,4096]{2,1,0:T(8,128)}) custom-call(s32[64]{0:T(128)S(1)} %copy-done.2, s32[64]{0:T(128)S(1)} %copy-done.1, bf16[128,48,128]{2,1,0:T(8,128)(2,1)S(1)} %get-tuple-element.24.returned_ref, f32[3,32,4096]{2,1,0:T(8,128)S(1)} %get-tuple-element.25.grid_ref), custom_call_target="tpu_custom_call" | custom-call | tf_op jit(solution)/shard_map/unpack/pallas_call | solution.py:732
Async XLA Ops:
  4.3 55.2 %copy-start = (f32[32,4096]{1,0:T(8,128)S(1)}, f32[32,4096]{1,0:T(8,128)}, u32[]{:S(2)}) copy-start(f32[32,4096]{1,0:T(8,128)} %drag_ref.1) | copy-start | bytes 1572868
  61.9 41.2 %copy-start.1 = (s32[64]{0:T(128)S(1)}, s32[64]{0:T(128)}, u32[]{:S(2)}) copy-start(s32[64]{0:T(128)} %count_ref.3) | copy-start | bytes 772
  61.9 41.2 %copy-start.2 = (s32[64]{0:T(128)S(1)}, s32[64]{0:T(128)}, u32[]{:S(2)}) copy-start(s32[64]{0:T(128)} %get-tuple-element.16.dest_ref) | copy-start | bytes 772
